TPU v7x, 128 devices: a whole 4x4x4 slice. The times are simulated.
128 devices in a mesh: row: 8 (over x, core), col: 16 (over z, y).
Axes of the slice: x: 4, y: 4, z: 4, core: 2. Of those that a mesh axis runs over, the one named last changes fastest.
Arguments:
- rhs: float32 [32, 1048576], P(None, ('row', 'col')), may hold values from -12.5 to 12.5
- near_blocks: bfloat16 [16384, 4, 4096], P(('row', 'col')), may hold values from -0.1875 to 0.1875
- near_offsets: int32 [16384, 4], P(('row', 'col')), may hold values from -4 to 4, as said below
- v_factor: bfloat16 [16384, 2048], P(('row', 'col')), may hold values from -0.75 to 0.75
- mix_col: bfloat16 [8, 128, 512, 512], P('row', 'col'), may hold values from -0.25 to 0.25
- mix_row: bfloat16 [8, 256, 256, 256], P('row', 'col'), may hold values from -0.375 to 0.375
- u_factor: bfloat16 [16384, 2048], P(('row', 'col')), may hold values from -0.75 to 0.75
Outputs:
- solution: float32 [32, 1048576], P(None, ('row', 'col'))
- residual: float32 [32, 1048576], P(None, ('row', 'col'))
Inputs may be any that keep to these rules, and one draw needn't show every extreme that they name: `near_offsets`: column 0 is 0; the other entries of a row are distinct and nonzero. In every aligned block of 128 rows some row holds -4 and some row holds 4.
All inputs are finite; a program needn't handle non-finite values.
Results may differ from a plain program's by a relative error of at most 0.0054.
Values may be sent and summed in bfloat16 or wider, within the bound.
A program may use at most 128 MiB of HBM per device.

v0:
```python
import functools

import jax
import jax.numpy as jnp
from jax import lax
from jax.sharding import Mesh
from jax.sharding import PartitionSpec as P

LEAF = 64
RANK = 32
HALO = 4
ROW_COL = ("row_0", "row_1", "col_0", "col_1")
ROW = ("row_0", "row_1")
COL = ("col_0", "col_1")


def extended(x, sides, width):
    edges = {}
    for axis, dim in sides:
        count, length = (lax.axis_size(axis), x.shape[dim])
        up = [(i, (i + 1) % count) for i in range(count - 1)]
        last = lax.slice_in_dim(x, length - width, length, axis=dim)
        first = lax.slice_in_dim(x, 0, width, axis=dim)
        edges[dim] = (
            lax.ppermute(last, axis, up),
            lax.ppermute(first, axis, [(b, a) for a, b in up]),
        )
    done = []
    for _, dim in sides:
        low, high = edges[dim]
        around = [(width, width) if d in done else (0, 0) for d in range(x.ndim)]
        x = jnp.concatenate([jnp.pad(low, around), x, jnp.pad(high, around)], axis=dim)
        done.append(dim)
    return x


def one_axis_at_a_time(x, axes):
    return functools.reduce(lax.psum, axes, x)


def near_part(vector_bf, near_blocks, near_offsets):
    count_rhs = vector_bf.shape[0]
    leaves = near_offsets.shape[0]
    blocks_per = near_offsets.shape[1]
    padded = extended(vector_bf, ((ROW_COL, 1),), HALO * LEAF)
    padded = padded.reshape(count_rhs, leaves + 2 * HALO, LEAF)
    position = jnp.arange(leaves, dtype=jnp.int32)[:, None] + near_offsets + HALO
    picked = padded[:, position, :]
    blocks = near_blocks.reshape(leaves, blocks_per, LEAF, LEAF)
    result = jnp.einsum("slnu,lnvu->slv", picked, blocks, preferred_element_type=jnp.float32)
    return result.reshape(count_rhs, leaves * LEAF)


def far_part(vector_bf, v_factor, mix_col, mix_row, u_factor):
    count_rhs = vector_bf.shape[0]
    n_row = lax.axis_size(ROW)
    n_col = lax.axis_size(COL)
    leaves = v_factor.shape[0]
    slots = leaves // n_col
    subslots = slots // n_row
    width_col = n_col * RANK
    width_row = n_row * RANK
    local = vector_bf.reshape(count_rhs, leaves, LEAF)
    coeffs = jnp.einsum(
        "slu,luk->lsk",
        local,
        v_factor.reshape(leaves, LEAF, RANK),
        preferred_element_type=jnp.float32,
    ).astype(jnp.bfloat16)
    grouped = coeffs.reshape(n_col, slots, count_rhs * RANK)
    received = lax.all_to_all(grouped, COL, split_axis=0, concat_axis=0, tiled=True)
    first = jnp.einsum(
        "cjsk,jckm->jsm",
        received.reshape(n_col, slots, count_rhs, RANK),
        mix_col.reshape(slots, n_col, RANK, width_col),
        preferred_element_type=jnp.float32,
    )
    first = first.astype(jnp.bfloat16)
    regrouped = lax.all_to_all(first, ROW, split_axis=0, concat_axis=0, tiled=True)
    regrouped = regrouped.reshape(n_row, subslots, count_rhs, n_col, RANK)
    second = jnp.einsum(
        "rjspk,jprkn->jpsn",
        regrouped,
        mix_row.reshape(subslots, n_col, n_row, RANK, width_row),
        preferred_element_type=jnp.float32,
    ).astype(jnp.bfloat16)
    second = second.reshape(subslots, n_col, count_rhs, n_row, RANK)
    expanded = jnp.einsum(
        "jpsqk,jpqku->sjpqu",
        second,
        u_factor.reshape(subslots, n_col, n_row, RANK, LEAF),
        preferred_element_type=jnp.float32,
    )
    return expanded.reshape(count_rhs, leaves * LEAF)


def orthogonal(bases, image):
    partial_sums = [jnp.sum(basis * image, axis=1) for basis in bases] + [
        jnp.sum(image * image, axis=1)
    ]
    joined = one_axis_at_a_time(jnp.stack(partial_sums), ROW_COL)
    sums = joined[:-1]
    rest = image
    for index_basis in range(len(bases)):
        rest = rest - sums[index_basis][:, None] * bases[index_basis]
    length = jnp.sqrt(joined[-1] - jnp.sum(sums * sums, axis=0))
    return (sums, rest, length)


def body(rhs, near_blocks, near_offsets, v_factor, mix_col, mix_row, u_factor):

    def operator(vector):
        vector_bf = vector.astype(jnp.bfloat16)
        return (
            vector
            + near_part(vector_bf, near_blocks, near_offsets)
            + far_part(vector_bf, v_factor, mix_col, mix_row, u_factor)
        )

    rhs_length = jnp.sqrt(one_axis_at_a_time(jnp.sum(rhs * rhs, axis=1), ROW_COL))
    basis_first = rhs / rhs_length[:, None]
    image_first = operator(basis_first)
    proj_first, rest_first, h_two_one = orthogonal((basis_first,), image_first)
    h_one_one = proj_first[0]
    basis_second = rest_first / h_two_one[:, None]
    image_second = operator(basis_second)
    proj_second, rest_second, h_three_two = orthogonal((basis_first, basis_second), image_second)
    h_one_two = proj_second[0]
    h_two_two = proj_second[1]
    m_first = h_one_one * h_one_one + h_two_one * h_two_one
    m_cross = h_one_one * h_one_two + h_two_one * h_two_two
    m_second = h_one_two * h_one_two + h_two_two * h_two_two + h_three_two * h_three_two
    determ = m_first * m_second - m_cross * m_cross
    coef_first = rhs_length * (m_second * h_one_one - m_cross * h_one_two) / determ
    coef_second = rhs_length * (m_first * h_one_two - m_cross * h_one_one) / determ
    solution = coef_first[:, None] * basis_first + coef_second[:, None] * basis_second
    residual = rhs - coef_first[:, None] * image_first - coef_second[:, None] * image_second
    return (solution, residual)


def solution(mesh):
    split = Mesh(mesh.devices.reshape(4, 2, 4, 4), ("row_0", "row_1", "col_0", "col_1"))
    return jax.shard_map(
        body,
        mesh=split,
        in_specs=(
            P(None, ROW_COL),
            P(ROW_COL, None, None),
            P(ROW_COL, None),
            P(ROW_COL, None),
            P(ROW, COL, None, None),
            P(ROW, COL, None, None),
            P(ROW_COL, None),
        ),
        out_specs=(P(None, ROW_COL), P(None, ROW_COL)),
        check_vma=False,
    )
```

profile of v0, /device:TPU:1, one launch (start us, length us, event | category | flops | bytes accessed | tf_op | source)
XLA Modules:
  0.0 281.8 jit_solution(2453957108290351879)
XLA Ops:
  2.2 9.3 %psum.84 = f32[32]{0:T(128)S(1)} all-reduce(f32[32]{0:T(128)S(1)} %multiply_reduce_fusion.5), channel_id=1, replica_groups=mesh['row_0'=4,'row_1'=2,'col_0'=4,'col_1'=4] {'row_0'}, use_global_device_ids=true, to_apply=%region_1.0 | all-reduce | flops 32 | bytes 256 | tf_op jit(solution)/shard_map/psum | solution.py:38
  11.5 4.8 %psum.85 = f32[32]{0:T(128)S(1)} all-reduce(f32[32]{0:T(128)S(1)} %psum.84), channel_id=1, replica_groups=mesh['row_0'=4,'row_1'=2,'col_0'=4,'col_1'=4] {'row_1'}, use_global_device_ids=true, to_apply=%region_2.0 | all-reduce | flops 32 | bytes 256 | tf_op jit(solution)/shard_map/psum | solution.py:38
  16.3 9.7 %psum.86 = f32[32]{0:T(128)S(1)} all-reduce(f32[32]{0:T(128)S(1)} %psum.85), channel_id=1, replica_groups=mesh['row_0'=4,'row_1'=2,'col_0'=4,'col_1'=4] {'col_0'}, use_global_device_ids=true, to_apply=%region_3.0 | all-reduce | flops 32 | bytes 256 | tf_op jit(solution)/shard_map/psum | solution.py:38
  26.0 8.7 %psum.87 = f32[32]{0:T(128)S(1)} all-reduce(f32[32]{0:T(128)S(1)} %psum.86), channel_id=1, replica_groups=mesh['row_0'=4,'row_1'=2,'col_0'=4,'col_1'=4] {'col_1'}, use_global_device_ids=true, to_apply=%region_4.0 | all-reduce | flops 32 | bytes 256 | tf_op jit(solution)/shard_map/psum | solution.py:38
  38.1 7.0 %collective-permute-start.1 = (bf16[32,256]{1,0:T(8,128)(2,1)S(1)}, bf16[32,256]{1,0:T(8,128)(2,1)S(1)}, u32[]{:S(2)}, u32[]{:S(2)}) collective-permute-start(bf16[32,256]{1,0:T(8,128)(2,1)S(1)} %get-tuple-element.16), channel_id=1, source_target_pairs={{1,0},{2,1},{3,2},{4,3},{5,4},{6,5},{7,6},{8,7},{9,8},{10,9},{11,1... | collective-permute-start | bytes 49160 | tf_op jit(solution)/shard_map/ppermute | solution.py:26
  48.1 2.8 copy.28
  51.0 3.4 %convolution_convert_fusion.1 = bf16[128,32,32]{2,1,0:T(8,128)(2,1)} fusion(bf16[128,64,32]{1,2,0:T(8,128)(2,1)S(1)} %copy.28, bf16[32,128,64]{2,1,0:T(8,128)(2,1)} %reshape.116), kind=kOutput, calls=%fused_computation.7 | convolution fusion | flops 16908288 | bytes 1310720 | tf_op jit(solution)/shard_map/slu,luk->lsk/dot_general | solution.py:64
  54.4 2.9 %reshape.118 = bf16[16,8,1024]{2,1,0:T(8,128)(2,1)} reshape(bf16[128,32,32]{2,1,0:T(8,128)(2,1)} %convolution_convert_fusion.1) | data formatting | bytes 524288 | tf_op jit(solution)/shard_map/reshape | solution.py:70
  57.3 4.5 %all-to-all-start = ((bf16[16,8,1024]{2,1,0:T(8,128)(2,1)}), bf16[16,8,1024]{2,1,0:T(8,128)(2,1)}, u32[]{:S(2)}, u32[]{:S(2)}) async-start(bf16[16,8,1024]{2,1,0:T(8,128)(2,1)} %reshape.118), calls=%async_computation | async-start | bytes 524288 | tf_op jit(solution)/shard_map/all_to_all | solution.py:71
  62.0 7.9 %copy.23 = bf16[128,4,4096]{0,2,1:T(8,128)(2,1)} copy(bf16[128,4,4096]{2,1,0:T(4,128)(2,1)} %param.8) | data formatting | bytes 8388608 | tf_op args[1]
  69.9 13.0 %copy.24 = bf16[128,4,64,64]{3,2,1,0:T(8,128)(2,1)} copy(bf16[128,4,64,64]{0,3,2,1:T(8,128)(2,1)} %bitcast.155) | data formatting | bytes 8388608 | tf_op jit(solution)/shard_map/reshape | solution.py:49
  87.2 2.6 reshape.113
  89.8 2.5 copy.22
  92.3 4.4 %gather_fusion = bf16[512,32,64]{2,1,0:T(8,128)(2,1)} fusion(bf16[32,136,64]{2,0,1:T(8,128)(2,1)} %copy.22, s32[1024]{0:T(1024)S(1)} %pad_clamp_fusion), kind=kCustom, calls=%fused_computation | custom fusion | bytes 4196352 | tf_op jit(solution)/shard_map/gather | solution.py:48
  99.6 4.3 %fusion = bf16[8,32,512]{2,1,0:T(8,128)(2,1)} fusion(bf16[16,8,32,32]{3,2,0,1:T(8,128)(2,1)} %reshape.119, bf16[8,16,32,512]{3,2,1,0:T(8,128)(2,1)} %bitcast.151), kind=kOutput, calls=%fused_computation.12 | convolution fusion | flops 134348800 | bytes 4718592 | tf_op jit(solution)/shard_map/cjsk,jckm->jsm/dot_general | solution.py:72
  103.9 7.1 %all-to-all-start.1 = ((bf16[8,32,512]{2,1,0:T(8,128)(2,1)}), bf16[8,32,512]{2,1,0:T(8,128)(2,1)S(1)}, u32[]{:S(2)}, u32[]{:S(2)}) async-start(bf16[8,32,512]{2,1,0:T(8,128)(2,1)} %fusion), calls=%async_computation.1 | async-start | bytes 524288 | tf_op jit(solution)/shard_map/all_to_all | solution.py:79
  111.0 6.9 %convolution_bitcast_fusion.1 = f32[32,128,64]{2,0,1:T(8,128)S(1)} fusion(bf16[32,128,4,64]{3,0,2,1:T(8,128)(2,1)} %bitcast.154, bf16[128,4,64,64]{3,2,1,0:T(8,128)(2,1)} %copy.24), kind=kOutput, calls=%fused_computation.3 | convolution fusion | flops 134217728 | bytes 7340032 | tf_op jit(solution)/shard_map/slnu,lnvu->slv/dot_general | solution.py:50
  117.9 2.6 copy.25
  120.5 2.9 %reshape.115 = f32[32,8192]{1,0:T(8,128)} reshape(f32[32,128,64]{2,1,0:T(8,128)} %copy.25) | data formatting | bytes 2097152 | tf_op jit(solution)/shard_map/reshape | solution.py:51
  129.9 2.6 copy.32
  132.5 3.0 %reshape.125 = f32[32,8192]{1,0:T(8,128)} reshape(f32[32,1,16,8,64]{4,3,2,0,1:T(8,128)} %copy.32) | data formatting | bytes 2097152 | tf_op jit(solution)/shard_map/reshape | solution.py:94
  135.4 2.9 %multiply_reduce_fusion.4 = (f32[32]{0:T(128)S(1)}, f32[32]{0:T(128)S(1)}, f32[32,8192]{1,0:T(8,128)}) fusion(f32[32,8192]{1,0:T(8,128)S(1)} %copy-done.1, f32[32]{0:T(128)S(1)} %sqrt.16, f32[32,8192]{1,0:T(8,128)} %reshape.125, f32[32,8192]{1,0:T(8,128)} %reshape.115), kind=kLoop, calls=%fused_computation.30 | loop fusion | flops 1834944 | bytes 4194688 | tf_op jit(solution)/shard_map/reduce_sum | solution.py:98
  138.4 8.6 %psum.88 = f32[2,32]{1,0:T(2,128)S(1)} all-reduce(f32[2,32]{1,0:T(2,128)S(1)} %pad_maximum_fusion.3), channel_id=1, replica_groups=mesh['row_0'=4,'row_1'=2,'col_0'=4,'col_1'=4] {'row_0'}, use_global_device_ids=true, to_apply=%region_7.8 | all-reduce | flops 64 | bytes 512 | tf_op jit(solution)/shard_map/psum | solution.py:38
  146.9 4.5 %psum.89 = f32[2,32]{1,0:T(2,128)S(1)} all-reduce(f32[2,32]{1,0:T(2,128)S(1)} %psum.88), channel_id=1, replica_groups=mesh['row_0'=4,'row_1'=2,'col_0'=4,'col_1'=4] {'row_1'}, use_global_device_ids=true, to_apply=%region_8.9 | all-reduce | flops 64 | bytes 512 | tf_op jit(solution)/shard_map/psum | solution.py:38
  151.5 8.7 %psum.90 = f32[2,32]{1,0:T(2,128)S(1)} all-reduce(f32[2,32]{1,0:T(2,128)S(1)} %psum.89), channel_id=1, replica_groups=mesh['row_0'=4,'row_1'=2,'col_0'=4,'col_1'=4] {'col_0'}, use_global_device_ids=true, to_apply=%region_9.10 | all-reduce | flops 64 | bytes 512 | tf_op jit(solution)/shard_map/psum | solution.py:38
  160.2 8.4 %psum.91 = f32[2,32]{1,0:T(2,128)S(1)} all-reduce(f32[2,32]{1,0:T(2,128)S(1)} %psum.90), channel_id=1, replica_groups=mesh['row_0'=4,'row_1'=2,'col_0'=4,'col_1'=4] {'col_1'}, use_global_device_ids=true, to_apply=%region_10.11 | all-reduce | flops 64 | bytes 512 | tf_op jit(solution)/shard_map/psum | solution.py:38
  168.6 2.5 fusion.22
  171.9 2.8 reshape.128
  176.6 7.0 %collective-permute-start.3 = (bf16[32,256]{1,0:T(8,128)(2,1)S(1)}, bf16[32,256]{1,0:T(8,128)(2,1)S(1)}, u32[]{:S(2)}, u32[]{:S(2)}) collective-permute-start(bf16[32,256]{1,0:T(8,128)(2,1)S(1)} %get-tuple-element.14), channel_id=1, source_target_pairs={{1,0},{2,1},{3,2},{4,3},{5,4},{6,5},{7,6},{8,7},{9,8},{10,9},{11,1... | collective-permute-start | bytes 49160 | tf_op jit(solution)/shard_map/ppermute | solution.py:26
  183.5 3.4 %convolution_convert_fusion = bf16[128,32,32]{2,1,0:T(8,128)(2,1)} fusion(bf16[128,64,32]{1,2,0:T(8,128)(2,1)} %copy-done.2, bf16[32,128,64]{2,1,0:T(8,128)(2,1)} %reshape.128), kind=kOutput, calls=%fused_computation.6 | convolution fusion | flops 16908288 | bytes 1310720 | tf_op jit(solution)/shard_map/slu,luk->lsk/dot_general | solution.py:64
  187.0 2.9 %reshape.129 = bf16[16,8,1024]{2,1,0:T(8,128)(2,1)} reshape(bf16[128,32,32]{2,1,0:T(8,128)(2,1)} %convolution_convert_fusion) | data formatting | bytes 524288 | tf_op jit(solution)/shard_map/reshape | solution.py:70
  189.9 4.5 %all-to-all-start.2 = ((bf16[16,8,1024]{2,1,0:T(8,128)(2,1)}), bf16[16,8,1024]{2,1,0:T(8,128)(2,1)}, u32[]{:S(2)}, u32[]{:S(2)}) async-start(bf16[16,8,1024]{2,1,0:T(8,128)(2,1)} %reshape.129), calls=%async_computation.2 | async-start | bytes 524288 | tf_op jit(solution)/shard_map/all_to_all | solution.py:71
  196.3 2.6 reshape.126
  198.9 2.5 copy.33
  201.4 4.4 %gather_fusion.1 = bf16[512,32,64]{2,1,0:T(8,128)(2,1)} fusion(bf16[32,136,64]{2,0,1:T(8,128)(2,1)} %copy.33, s32[1024]{0:T(1024)S(1)} %pad_clamp_fusion), kind=kCustom, calls=%fused_computation.1 | custom fusion | bytes 4196352 | tf_op jit(solution)/shard_map/gather | solution.py:48
  208.7 4.3 %fusion.1 = bf16[8,32,512]{2,1,0:T(8,128)(2,1)} fusion(bf16[16,8,32,32]{3,2,0,1:T(8,128)(2,1)} %reshape.130, bf16[8,16,32,512]{3,2,1,0:T(8,128)(2,1)} %bitcast.152), kind=kOutput, calls=%fused_computation.13 | convolution fusion | flops 134348800 | bytes 4718592 | tf_op jit(solution)/shard_map/cjsk,jckm->jsm/dot_general | solution.py:72
  213.0 7.3 %all-to-all-start.3 = ((bf16[8,32,512]{2,1,0:T(8,128)(2,1)}), bf16[8,32,512]{2,1,0:T(8,128)(2,1)S(1)}, u32[]{:S(2)}, u32[]{:S(2)}) async-start(bf16[8,32,512]{2,1,0:T(8,128)(2,1)} %fusion.1), calls=%async_computation.3 | async-start | bytes 524288 | tf_op jit(solution)/shard_map/all_to_all | solution.py:79
  220.3 6.9 %convolution_bitcast_fusion = f32[32,128,64]{2,0,1:T(8,128)S(1)} fusion(bf16[32,128,4,64]{3,0,2,1:T(8,128)(2,1)} %bitcast.153, bf16[128,4,64,64]{3,2,1,0:T(8,128)(2,1)} %copy.24), kind=kOutput, calls=%fused_computation.2 | convolution fusion | flops 134217728 | bytes 7340032 | tf_op jit(solution)/shard_map/slnu,lnvu->slv/dot_general | solution.py:50
  227.2 2.6 copy.35
  229.8 2.9 %reshape.127 = f32[32,8192]{1,0:T(8,128)} reshape(f32[32,128,64]{2,1,0:T(8,128)} %copy.35) | data formatting | bytes 2097152 | tf_op jit(solution)/shard_map/reshape | solution.py:51
  239.5 2.6 copy.41
  242.1 2.9 %reshape.133 = f32[32,8192]{1,0:T(8,128)} reshape(f32[32,1,16,8,64]{4,3,2,0,1:T(8,128)} %copy.41) | data formatting | bytes 2097152 | tf_op jit(solution)/shard_map/reshape | solution.py:94
  245.0 3.3 %multiply_reduce_fusion.2 = (f32[32]{0:T(128)S(1)}, f32[32]{0:T(128)S(1)}, f32[32]{0:T(128)S(1)}, f32[32,8192]{1,0:T(8,128)}) fusion(f32[32,8192]{1,0:T(8,128)S(1)} %copy-done.1, f32[32]{0:T(128)S(1)} %sqrt.16, f32[32,8192]{1,0:T(8,128)} %get-tuple-element.9, f32[32,8192]{1,0:T(8,128)} %reshape.133, f32[32,8192]{1,0:T(8,128)} %reshape.127), kind=kLoop, calls=%fused_computation.26 | loop fusion | flops 2359200 | bytes 5243392 | tf_op jit(solution)/shard_map/reduce_sum | solution.py:98
  248.3 8.6 %psum.92 = f32[3,32]{1,0:T(4,128)S(1)} all-reduce(f32[3,32]{1,0:T(4,128)S(1)} %pad_maximum_fusion.2), channel_id=1, replica_groups=mesh['row_0'=4,'row_1'=2,'col_0'=4,'col_1'=4] {'row_0'}, use_global_device_ids=true, to_apply=%region_14.15 | all-reduce | flops 96 | bytes 768 | tf_op jit(solution)/shard_map/psum | solution.py:38
  256.9 4.5 %psum.93 = f32[3,32]{1,0:T(4,128)S(1)} all-reduce(f32[3,32]{1,0:T(4,128)S(1)} %psum.92), channel_id=1, replica_groups=mesh['row_0'=4,'row_1'=2,'col_0'=4,'col_1'=4] {'row_1'}, use_global_device_ids=true, to_apply=%region_15.16 | all-reduce | flops 96 | bytes 768 | tf_op jit(solution)/shard_map/psum | solution.py:38
  261.4 8.5 %psum.94 = f32[3,32]{1,0:T(4,128)S(1)} all-reduce(f32[3,32]{1,0:T(4,128)S(1)} %psum.93), channel_id=1, replica_groups=mesh['row_0'=4,'row_1'=2,'col_0'=4,'col_1'=4] {'col_0'}, use_global_device_ids=true, to_apply=%region_16.17 | all-reduce | flops 96 | bytes 768 | tf_op jit(solution)/shard_map/psum | solution.py:38
  269.9 8.4 %psum.95 = f32[3,32]{1,0:T(4,128)S(1)} all-reduce(f32[3,32]{1,0:T(4,128)S(1)} %psum.94), channel_id=1, replica_groups=mesh['row_0'=4,'row_1'=2,'col_0'=4,'col_1'=4] {'col_1'}, use_global_device_ids=true, to_apply=%region_17.18 | all-reduce | flops 96 | bytes 768 | tf_op jit(solution)/shard_map/psum | solution.py:38
  278.3 3.5 %multiply_subtract_fusion = (f32[32,8192]{1,0:T(8,128)}, f32[32,8192]{1,0:T(8,128)}) fusion(f32[32,8192]{1,0:T(8,128)} %get-tuple-element.7, f32[32,8192]{1,0:T(8,128)S(1)} %copy-done.1, f32[32,8192]{1,0:T(8,128)} %get-tuple-element.10, f32[32]{0:T(128)S(1)} %get-tuple-element.18, f32[32]{0:T(128)S(1)} %get-tuple-element.17, ...), kind=kLoop, calls=%fused_computation.22 | loop fusion | flops 2097152 | bytes 6291840 | tf_op jit(solution)/shard_map/sub | solution.py:137
  (57 shorter events, 36.2 us)
Async XLA Ops:
  0.6 124.4 %copy-start = (bf16[1,16,256,256]{3,2,1,0:T(8,128)(2,1)S(1)}, bf16[1,16,256,256]{3,2,1,0:T(8,128)(2,1)}, u32[]{:S(2)}) copy-start(bf16[1,16,256,256]{3,2,1,0:T(8,128)(2,1)} %param.12) | copy-start | bytes 6291460
  0.6 46.5 %copy-start.6 = (bf16[128,2048]{1,0:T(8,128)(2,1)S(1)}, bf16[128,2048]{1,0:T(8,128)(2,1)}, u32[]{:S(2)}) copy-start(bf16[128,2048]{1,0:T(8,128)(2,1)} %param.10) | copy-start | bytes 1572868
  36.1 12.0 %copy-start.4 = (bf16[32,8192]{1,0:T(8,128)(2,1)}, bf16[32,8192]{1,0:T(8,128)(2,1)S(1)}, u32[]{:S(2)}) copy-start(bf16[32,8192]{1,0:T(8,128)(2,1)S(1)} %fusion.21) | copy-start | bytes 1572868
  36.1 48.8 %collective-permute-start = (bf16[32,256]{1,0:T(8,128)(2,1)S(1)}, bf16[32,256]{1,0:T(8,128)(2,1)S(1)}, u32[]{:S(2)}, u32[]{:S(2)}) collective-permute-start(bf16[32,256]{1,0:T(8,128)(2,1)S(1)} %get-tuple-element.15), channel_id=1, source_target_pairs={{0,1},{1,2},{2,3},{3,4},{4,5},{5,6},{6,7},{7,8},{8,9},{9,10},{10,1... | collective-permute-start | bytes 49160 | tf_op jit(solution)/shard_map/ppermute | solution.py:25
  38.1 46.9 %collective-permute-start.1 = (bf16[32,256]{1,0:T(8,128)(2,1)S(1)}, bf16[32,256]{1,0:T(8,128)(2,1)S(1)}, u32[]{:S(2)}, u32[]{:S(2)}) collective-permute-start(bf16[32,256]{1,0:T(8,128)(2,1)S(1)} %get-tuple-element.16), channel_id=1, source_target_pairs={{1,0},{2,1},{3,2},{4,3},{5,4},{6,5},{7,6},{8,7},{9,8},{10,9},{11,1... | collective-permute-start | bytes 49160 | tf_op jit(solution)/shard_map/ppermute | solution.py:26
  50.9 6.3 %copy-start.2 = (bf16[128,64,32]{1,2,0:T(8,128)(2,1)}, bf16[128,64,32]{1,2,0:T(8,128)(2,1)S(1)}, u32[]{:S(2)}) copy-start(bf16[128,64,32]{1,2,0:T(8,128)(2,1)S(1)} %copy.28) | copy-start | bytes 1572868
  51.0 10.8 %copy-start.7 = (s32[128,4]{0,1:T(4,128)S(1)}, s32[128,4]{0,1:T(4,128)}, u32[]{:S(2)}) copy-start(s32[128,4]{0,1:T(4,128)} %param.9) | copy-start | bytes 6148
  57.3 39.5 %all-to-all-start = ((bf16[16,8,1024]{2,1,0:T(8,128)(2,1)}), bf16[16,8,1024]{2,1,0:T(8,128)(2,1)}, u32[]{:S(2)}, u32[]{:S(2)}) async-start(bf16[16,8,1024]{2,1,0:T(8,128)(2,1)} %reshape.118), calls=%async_computation | async-start | bytes 524288 | tf_op jit(solution)/shard_map/all_to_all | solution.py:71
  84.9 43.3 %copy-start.3 = (bf16[16,8,32,64]{3,2,1,0:T(8,128)(2,1)}, bf16[16,8,32,64]{3,2,1,0:T(8,128)(2,1)S(1)}, u32[]{:S(2)}) copy-start(bf16[16,8,32,64]{3,2,1,0:T(8,128)(2,1)S(1)} %reshape.124) | copy-start | bytes 1572868
  103.9 19.6 %all-to-all-start.1 = ((bf16[8,32,512]{2,1,0:T(8,128)(2,1)}), bf16[8,32,512]{2,1,0:T(8,128)(2,1)S(1)}, u32[]{:S(2)}, u32[]{:S(2)}) async-start(bf16[8,32,512]{2,1,0:T(8,128)(2,1)} %fusion), calls=%async_computation.1 | async-start | bytes 524288 | tf_op jit(solution)/shard_map/all_to_all | solution.py:79
  132.5 3.0 %copy-start.1 = (f32[32,8192]{1,0:T(8,128)S(1)}, f32[32,8192]{1,0:T(8,128)}, u32[]{:S(2)}) copy-start(f32[32,8192]{1,0:T(8,128)} %param.7) | copy-start | bytes 3145732
  171.1 0.8 copy-start.5
  174.6 19.7 %collective-permute-start.2 = (bf16[32,256]{1,0:T(8,128)(2,1)S(1)}, bf16[32,256]{1,0:T(8,128)(2,1)S(1)}, u32[]{:S(2)}, u32[]{:S(2)}) collective-permute-start(bf16[32,256]{1,0:T(8,128)(2,1)S(1)} %get-tuple-element.13), channel_id=1, source_target_pairs={{0,1},{1,2},{2,3},{3,4},{4,5},{5,6},{6,7},{7,8},{8,9},{9,10},{10,1... | collective-permute-start | bytes 49160 | tf_op jit(solution)/shard_map/ppermute | solution.py:25
  176.6 17.8 %collective-permute-start.3 = (bf16[32,256]{1,0:T(8,128)(2,1)S(1)}, bf16[32,256]{1,0:T(8,128)(2,1)S(1)}, u32[]{:S(2)}, u32[]{:S(2)}) collective-permute-start(bf16[32,256]{1,0:T(8,128)(2,1)S(1)} %get-tuple-element.14), channel_id=1, source_target_pairs={{1,0},{2,1},{3,2},{4,3},{5,4},{6,5},{7,6},{8,7},{9,8},{10,9},{11,1... | collective-permute-start | bytes 49160 | tf_op jit(solution)/shard_map/ppermute | solution.py:26
  189.9 15.9 %all-to-all-start.2 = ((bf16[16,8,1024]{2,1,0:T(8,128)(2,1)}), bf16[16,8,1024]{2,1,0:T(8,128)(2,1)}, u32[]{:S(2)}, u32[]{:S(2)}) async-start(bf16[16,8,1024]{2,1,0:T(8,128)(2,1)} %reshape.129), calls=%async_computation.2 | async-start | bytes 524288 | tf_op jit(solution)/shard_map/all_to_all | solution.py:71
  213.0 19.7 %all-to-all-start.3 = ((bf16[8,32,512]{2,1,0:T(8,128)(2,1)}), bf16[8,32,512]{2,1,0:T(8,128)(2,1)S(1)}, u32[]{:S(2)}, u32[]{:S(2)}) async-start(bf16[8,32,512]{2,1,0:T(8,128)(2,1)} %fusion.1), calls=%async_computation.3 | async-start | bytes 524288 | tf_op jit(solution)/shard_map/all_to_all | solution.py:79
where the time goes:
time: 287 us; the launch traced here: 282 us
  blocking collectives  92.7 us (32%)
  local copies, waits for them, and re-layouts  91.4 us (32%)
  starting transfers between devices  41.1 us (14%)
  matrix products  36.4 us (13%)
  other arithmetic  19.3 us (7%)
    psum x12, blocking collectives, one_axis_at_a_time(): return functools.reduce(lax.psum, axes, x)  92.7 us
    all_to_all x2, starting transfers between devices, far_part(): lax.all_to_all(first, ROW, split_axis=0, concat_axis=0, tiled=True)  14.4 us
    ppermute x2, starting transfers between devices, extended(): lax.ppermute(first, axis, [(b, a) for a, b in up])  13.9 us
    dot_general x2, matrix products, near_part(): jnp.einsum('slnu,lnvu->slv', picked, blocks, preferred_element_type=jnp.f...  13.9 us
    reshape x1, local copies, waits for them, and re-layouts, near_part(): blocks = near_blocks.reshape(leaves, blocks_per, LEAF, LEAF)  13 us
    reshape x4, local copies, waits for them, and re-layouts, near_part(): padded = padded.reshape(count_rhs, leaves + 2 * HALO, LEAF)  10.2 us
    unnamed x18, local copies, waits for them, and re-layouts  9.72 us
    all_to_all x2, starting transfers between devices, far_part(): lax.all_to_all(grouped, COL, split_axis=0, concat_axis=0, tiled=True)  8.99 us
  transfers between devices with their start and end apart: 8, of which 0 were waited for; matrix products, arithmetic and copies ran while one was open for 32% of the time, Pallas kernels for 0%

commit v1 on v0

v1 whole, which is shorter than its diff:
```python
import functools

import jax
import jax.numpy as jnp
from jax import lax
from jax.experimental import pallas as pl
from jax.experimental.pallas import tpu as pltpu
from jax.sharding import PartitionSpec as P

S = 32
LEAF = 64
RANK = 32
HALO = 4
F32 = jnp.float32
BF16 = jnp.bfloat16
MESH = pl.DeviceIdType.MESH
NT = (((1,), (1,)), ((), ()))


def dot(a, b):
    return jnp.dot(a, b, preferred_element_type=F32)


def lane_index():
    return lax.broadcasted_iota(jnp.int32, (S, 128), 1)


def blocks_swapped(tiles):
    lane = lane_index()
    low_half = lane < 64
    low_quarter = lax.rem(lane, 64) < 32
    a, b, c, d = tiles
    turn = lambda x, by: pltpu.roll(x, by, 1)
    a, c = jnp.where(low_half, a, turn(c, 64)), jnp.where(low_half, turn(a, 64), c)
    b, d = jnp.where(low_half, b, turn(d, 64)), jnp.where(low_half, turn(b, 64), d)
    a, b = jnp.where(low_quarter, a, turn(b, 32)), jnp.where(low_quarter, turn(a, 96), b)
    c, d = jnp.where(low_quarter, c, turn(d, 32)), jnp.where(low_quarter, turn(c, 96), d)
    return a, b, c, d


def kernel(
    n_row, n_col,
    r_hbm, w_hbm, off, v_hbm, mc_hbm, mr_hbm, u_hbm,
    sol, res,
    rv, bv, dv, wraw, wp, vraw, vq, uraw, uq, mc, mr, xlo, xhi,
    hs, hr, zs, zr, zt, ts, tr, tt, sa, sb, g1, h1, g2, h2,
    load_sem, hs_sem, hr_sem, zs_sem, zr_sem, ts_sem, tr_sem, g_sem, h_sem,
):
    row = lax.axis_index("row")
    col = lax.axis_index("col")
    flat = row * n_col + col
    total = n_row * n_col
    leaves = off.shape[1]
    lane = lane_index()
    low_half = lane < 64

    def loads(index, src, dst):
        copy = pltpu.make_async_copy(src, dst, load_sem.at[index])
        copy.start()
        return copy

    v_load = loads(0, v_hbm, vraw)
    r_load = loads(1, r_hbm, rv)
    w_load = loads(2, w_hbm, wraw)
    mc_load = loads(3, mc_hbm, mc)
    mr_load = loads(4, mr_hbm, mr)
    u_load = loads(5, u_hbm, uraw)

    def other_col(k):
        return lax.rem(col + k, n_col)

    def other_row(k):
        return lax.rem(row + k, n_row)

    def at_flat(k):
        other = lax.rem(flat + k, total)
        return (lax.div(other, n_col), lax.rem(other, n_col))

    up, down = at_flat(1), at_flat(total - 1)
    barrier = pltpu.get_barrier_semaphore()
    partners = [(row, other_col(k)) for k in range(1, n_col)]
    partners += [(other_row(k), col) for k in range(1, n_row)] + [up, down]
    for partner in partners:
        pl.semaphore_signal(barrier, inc=1, device_id=partner, device_id_type=MESH)

    sends = []

    def send(src, dst, send_sem, recv_sem, device):
        copy = pltpu.make_async_remote_copy(
            src_ref=src, dst_ref=dst, send_sem=send_sem, recv_sem=recv_sem,
            device_id=device, device_id_type=MESH,
        )
        copy.start()
        sends.append(copy)

    def arrived(dst, send_sem, recv_sem):
        pltpu.make_async_remote_copy(
            src_ref=dst, dst_ref=dst, send_sem=send_sem, recv_sem=recv_sem,
            device_id=(row, col), device_id_type=MESH,
        ).wait_recv()

    def expand_v():
        group = lax.broadcasted_iota(jnp.int32, (16, 128), 1) // RANK

        def step(at, _):
            sa[0] = vraw[pl.ds(pl.multiple_of(at * 128, 128), 128), :].astype(F32)
            for leaf in range(8):
                j = leaf % 4
                part = sa[0, pl.ds(leaf, 16, stride=8), :]
                for w in range(4):
                    turned = part if j == w else pltpu.roll(part, ((j - w) % 4) * RANK, 1)
                    sb[2 * (leaf // 4) + j // 2, pl.ds((j % 2) * 64 + w, 16, stride=4), :] = jnp.where(
                        group == j, turned, 0.0
                    )
            for q in range(4):
                vq[pl.ds(pl.multiple_of(at * 512 + q * 128, 128), 128), :] = sb[q].astype(BF16)
            return 0

        lax.fori_loop(0, leaves // 8, step, 0)

    def expand_u():
        half = lax.broadcasted_iota(jnp.int32, (16, 128), 1) // LEAF
        nothing = jnp.zeros((64, 128), BF16)

        def step(at, _):
            sa[0] = uraw[pl.ds(pl.multiple_of(at * 128, 128), 128), :].astype(F32)
            for leaf in range(8):
                q = leaf % 4
                part = sa[0, pl.ds(leaf, 16, stride=8), :]
                turned = pltpu.roll(part, 64, 1)
                for w in range(2):
                    sb[leaf // 4, pl.ds(q * RANK + w, 16, stride=2), :] = jnp.where(
                        half == q % 2, part if w == q % 2 else turned, 0.0
                    )
            for q in range(2):
                base = pl.multiple_of(at * 256 + q * 128, 128)
                uq[pl.ds(base, 64), 0:128] = sb[q, 0:64].astype(BF16)
                uq[pl.ds(base, 64), 128:256] = nothing
                uq[pl.ds(base + 64, 64), 0:128] = nothing
                uq[pl.ds(base + 64, 64), 128:256] = sb[q, 64:128].astype(BF16)
            return 0

        lax.fori_loop(0, leaves // 8, step, 0)

    def expand_w(first, last):
        half = lax.broadcasted_iota(jnp.int32, (32, 128), 1) < 64

        def step(at, _):
            for k in range(4):
                leaf = at * 4 + k
                sa[k] = wraw[pl.ds(pl.multiple_of(leaf * 128, 128), 128), :].astype(F32)
            for k in range(4):
                leaf = at * 4 + k
                for b in range(2):
                    one = sa[k, pl.ds(2 * b, 32, stride=4), :]
                    two = sa[k, pl.ds(2 * b + 1, 32, stride=4), :]
                    sb[k, pl.ds(64 * b, 32, stride=2), :] = jnp.where(half, one, pltpu.roll(two, 64, 1))
                    sb[k, pl.ds(64 * b + 1, 32, stride=2), :] = jnp.where(half, pltpu.roll(one, 64, 1), two)
            for k in range(4):
                base = pl.multiple_of((at * 4 + k) * 64, 64)
                wp[pl.ds(base, 64), 0:128] = sb[k, 0:64].astype(BF16)
                wp[pl.ds(base, 64), 128:256] = sb[k, 64:128].astype(BF16)
            return 0

        lax.fori_loop(first, last, step, 0)

    def send_edges(app, src):
        hs[app, 0] = src[:, 0 : HALO * LEAF].astype(BF16)
        hs[app, 1] = src[:, (leaves - HALO) * LEAF : leaves * LEAF].astype(BF16)
        send(hs.at[app, 0], hr.at[app, 1], hs_sem.at[app, 0], hr_sem.at[app, 1], down)
        send(hs.at[app, 1], hr.at[app, 0], hs_sem.at[app, 1], hr_sem.at[app, 0], up)

    def compress(app, src, k_range):
        outs = []
        for k in k_range:
            to = other_col(k)
            for q in range(2):
                base = pl.multiple_of((to * 2 + q) * 256, 256)
                x = src[:, pl.ds(base, 256)].astype(BF16)
                outs.append((k, to, q, dot(x, vq[pl.ds(base, 256), :]).astype(BF16)))
        for k, to, q, z in outs:
            if k:
                zs[app, to, q] = z
            else:
                zr[app, col, q] = z
        for k in k_range:
            if k:
                to = other_col(k)
                send(zs.at[app, to], zr.at[app, col], zs_sem.at[app, to], zr_sem.at[app, col], (row, to))

    def put_leaves(at, x):
        turned = pltpu.roll(x, 64, 1)
        zero = jnp.zeros_like(x)
        xlo[at] = jnp.where(low_half, x, zero).astype(BF16)
        xhi[at] = jnp.where(low_half, zero, turned).astype(BF16)
        xlo[at + 1] = jnp.where(low_half, turned, zero).astype(BF16)
        xhi[at + 1] = jnp.where(low_half, zero, x).astype(BF16)

    def spread(src):
        def step(at, _):
            for k in range(4):
                pair = at * 4 + k
                put_leaves(HALO + 2 * pair, src[:, pl.ds(pl.multiple_of(pair * 128, 128), 128)])
            return 0

        lax.fori_loop(0, leaves // 8, step, 0)

    def spread_edges(app):
        for side, inside in ((0, flat > 0), (1, flat < total - 1)):
            arrived(hr.at[app, side], hs_sem.at[app, side], hr_sem.at[app, side])
            for pair in range(HALO // 2):
                x = hr[app, side, :, pair * 128 : (pair + 1) * 128].astype(F32)
                x = jnp.where(inside, x, jnp.zeros_like(x))
                put_leaves(side * (HALO + leaves) + 2 * pair, x)

    def near(dst, first, last):
        def step(at, _):
            for k in range(2):
                pair = at * 2 + k
                parts = []
                for leaf in (2 * pair, 2 * pair + 1):
                    index = [leaf + HALO + off[b, leaf] for b in range(4)]
                    parts.append(
                        jnp.concatenate(
                            [xlo[index[0]] + xhi[index[1]], xlo[index[2]] + xhi[index[3]]], axis=1
                        )
                    )
                lhs = jnp.concatenate(parts, axis=0)
                out = lax.dot_general(
                    lhs, wp[pl.ds(pl.multiple_of(pair * 128, 128), 128), :], NT, preferred_element_type=F32
                )
                dst[:, pl.ds(pl.multiple_of(pair * 128, 128), 128)] = jnp.where(low_half, out[:S], out[S:])
            return 0

        lax.fori_loop(first, last, step, 0)

    def mix_columns(app):
        for k in range(1, n_col):
            source = other_col(k)
            arrived(zr.at[app, source], zs_sem.at[app, source], zr_sem.at[app, source])
        for half in range(2):
            for c in range(n_col // 4):
                tiles = [zr[app, 4 * c + i, half].astype(F32) for i in range(4)]
                for j, tile in enumerate(blocks_swapped(tiles)):
                    zt[4 * half + j, :, 128 * c : 128 * (c + 1)] = tile.astype(BF16)
        for k in list(range(1, n_row)) + [0]:
            j = other_row(k)
            t = dot(zt[j], mc[j]).astype(BF16)
            if k:
                ts[app, j] = t
                send(ts.at[app, j], tr.at[app, row], ts_sem.at[app, j], tr_sem.at[app, row], (j, col))
            else:
                tr[app, row] = t

    def mix_rows(app):
        for k in range(1, n_row):
            source = other_row(k)
            arrived(tr.at[app, source], ts_sem.at[app, source], tr_sem.at[app, source])
        for p in range(n_col // 4):
            for r in range(n_row // 4):
                tiles = [tr[app, 4 * r + i, :, 128 * p : 128 * (p + 1)].astype(F32) for i in range(4)]
                for j, tile in enumerate(blocks_swapped(tiles)):
                    tt[4 * p + j, :, 128 * r : 128 * (r + 1)] = tile.astype(BF16)

    def expand(dst, sums):
        def step(at, carry):
            for k in range(2):
                p = at * 2 + k
                t = dot(tt[p], mr[p])
                high = t.astype(BF16)
                for q in range(2):
                    base = pl.multiple_of((2 * p + q) * 256, 256)
                    weights = uq[pl.ds(pl.multiple_of((2 * p + q) * 128, 128), 128), :]
                    far = dot(high[:, 128 * q : 128 * (q + 1)], weights)
                    for part in range(2):
                        lanes = pl.ds(pl.multiple_of(base + part * 128, 128), 128)
                        out = dst[:, lanes] + far[:, part * 128 : (part + 1) * 128]
                        dst[:, lanes] = out
                        if sums:
                            rx, bx = rv[:, lanes], bv[:, lanes]
                            carry = (carry[0] + rx * out, carry[1] + bx * out, carry[2] + out * out)
            return carry

        zero = jnp.zeros((S, 128), F32)
        return lax.fori_loop(0, n_col // 2, step, (zero, zero, zero) if sums else 0)

    def early_sums():
        def step(at, carry):
            for k in range(4):
                lanes = pl.ds(pl.multiple_of((at * 4 + k) * 128, 128), 128)
                rx, bx = rv[:, lanes], bv[:, lanes]
                carry = (carry[0] + rx * rx, carry[1] + rx * bx, carry[2] + bx * bx)
            return carry

        zero = jnp.zeros((S, 128), F32)
        return lax.fori_loop(0, leaves // 8, step, (zero, zero, zero))

    groups = [list(range(1, 6)), list(range(6, 11)), list(range(11, n_col)) + [0]]

    v_load.wait()
    expand_v()
    r_load.wait()
    pl.semaphore_wait(barrier, len(partners))
    send_edges(0, rv)
    for group in groups:
        compress(0, rv, group)
    spread(rv)
    w_load.wait()
    expand_w(0, leaves // 4)
    spread_edges(0)
    mc_load.wait()
    mix_columns(0)
    u_load.wait()
    expand_u()
    near(bv, 0, leaves // 4)
    mr_load.wait()
    mix_rows(0)
    expand(bv, False)

    send_edges(1, bv)
    for group in groups:
        compress(1, bv, group)
    spread(bv)
    rr, rb, bb = early_sums()
    spread_edges(1)
    near(dv, 0, leaves // 8)
    mix_columns(1)
    near(dv, leaves // 8, leaves // 4)
    mix_rows(1)
    rd, bd, dd = expand(dv, True)

    small = lax.broadcasted_iota(jnp.int32, (8, 128), 1)
    packed = jnp.zeros((8, 128), F32)
    for q, products in enumerate((rr, rb, bb, rd, bd, dd)):
        column = jnp.sum(products, axis=1, keepdims=True)
        for g in range(S // 8):
            packed = jnp.where(small == 8 * g + q, column[8 * g : 8 * (g + 1)], packed)
    g1[...] = packed
    h1[row] = packed
    for k in range(1, n_row):
        to = other_row(k)
        send(g1, h1.at[row], g_sem.at[to], h_sem.at[row], (to, col))
    for k in range(1, n_row):
        source = other_row(k)
        arrived(h1.at[source], g_sem.at[source], h_sem.at[source])
    packed = h1[0]
    for k in range(1, n_row):
        packed = packed + h1[k]
    g2[...] = packed
    h2[col] = packed
    for k in range(1, n_col):
        to = other_col(k)
        send(g2, h2.at[col], g_sem.at[n_row + to], h_sem.at[n_row + col], (row, to))
    for k in range(1, n_col):
        source = other_col(k)
        arrived(h2.at[source], g_sem.at[n_row + source], h_sem.at[n_row + source])
    packed = h2[0]
    for k in range(1, n_col):
        packed = packed + h2[k]

    def of(q):
        return jnp.concatenate([packed[:, 8 * g + q : 8 * g + q + 1] for g in range(S // 8)], axis=0)

    rr, rb, bb, rd, bd, dd = (of(q) for q in range(6))
    inv = 1.0 / rr
    shift = rb * inv
    h21s = bb * inv - shift * shift
    h21 = jnp.sqrt(h21s)
    h11 = 1.0 + shift
    h12 = (rd - shift * rb) * inv / h21
    k22 = (bd - shift * bb - shift * rd + shift * shift * rb) * inv / h21s
    size = (dd - 2.0 * shift * bd + shift * shift * bb) * inv / h21s
    h32s = size - h12 * h12 - k22 * k22
    h22 = 1.0 + k22
    m11 = h11 * h11 + h21s
    m12 = h11 * h12 + h21 * h22
    m22 = h12 * h12 + h22 * h22 + h32s
    det = m11 * m22 - m12 * m12
    y1 = (m22 * h11 - m12 * h12) / det
    y2 = (m11 * h12 - m12 * h11) / det / h21
    wide = lambda x: jnp.broadcast_to(x, (S, 128))
    sol_r, sol_b = wide(y1 - y2 * shift), wide(y2)
    res_r, res_b = wide(1.0 - y1 + y2 * shift), wide(y1 + y2 - y2 * shift)

    def finish(at, _):
        for k in range(4):
            lanes = pl.ds(pl.multiple_of((at * 4 + k) * 128, 128), 128)
            r, b, d = rv[:, lanes], bv[:, lanes], dv[:, lanes]
            sol[:, lanes] = sol_r * r + sol_b * b
            res[:, lanes] = res_r * r - res_b * b - sol_b * d
        return 0

    lax.fori_loop(0, leaves // 8, finish, 0)
    for copy in sends:
        copy.wait_send()


def solution(mesh):
    n_row, n_col = mesh.shape["row"], mesh.shape["col"]

    def body(rhs, near_blocks, near_offsets, v_factor, mix_col, mix_row, u_factor):
        leaves = near_offsets.shape[0]
        unknowns = leaves * LEAF
        w = near_blocks.reshape(leaves, 4, 32, 128).transpose(0, 2, 1, 3).reshape(leaves * 128, 128)
        by_tile = lambda x: x.reshape(leaves // 8, 8, 16, 128).transpose(0, 2, 1, 3).reshape(leaves * 16, 128)
        any_spec = pl.BlockSpec(memory_space=pl.ANY)
        field = pltpu.VMEM((S, unknowns), F32)
        return pl.pallas_call(
            functools.partial(kernel, n_row, n_col),
            out_shape=[jax.ShapeDtypeStruct((S, unknowns), F32)] * 2,
            in_specs=[any_spec, any_spec, pl.BlockSpec(memory_space=pltpu.SMEM)] + [any_spec] * 4,
            out_specs=[pl.BlockSpec(memory_space=pltpu.VMEM)] * 2,
            scratch_shapes=[
                field, field, field,
                pltpu.VMEM((leaves * 128, 128), BF16),
                pltpu.VMEM((leaves * 64, 256), BF16),
                pltpu.VMEM((leaves * 16, 128), BF16),
                pltpu.VMEM((leaves * 64, 128), BF16),
                pltpu.VMEM((leaves * 16, 128), BF16),
                pltpu.VMEM((leaves * 32, 256), BF16),
                pltpu.VMEM(mix_col.shape[1:], BF16),
                pltpu.VMEM(mix_row.shape[1:], BF16),
                pltpu.VMEM((leaves + 2 * HALO, S, 128), BF16),
                pltpu.VMEM((leaves + 2 * HALO, S, 128), BF16),
                pltpu.VMEM((2, 2, S, HALO * LEAF), BF16),
                pltpu.VMEM((2, 2, S, HALO * LEAF), BF16),
                pltpu.VMEM((2, n_col, 2, S, 128), BF16),
                pltpu.VMEM((2, n_col, 2, S, 128), BF16),
                pltpu.VMEM((n_row, S, n_col * RANK), BF16),
                pltpu.VMEM((2, n_row, S, n_col * RANK), BF16),
                pltpu.VMEM((2, n_row, S, n_col * RANK), BF16),
                pltpu.VMEM((n_col, S, n_row * RANK), BF16),
                pltpu.VMEM((4, 128, 128), F32),
                pltpu.VMEM((4, 128, 128), F32),
                pltpu.VMEM((8, 128), F32),
                pltpu.VMEM((n_row, 8, 128), F32),
                pltpu.VMEM((8, 128), F32),
                pltpu.VMEM((n_col, 8, 128), F32),
                pltpu.SemaphoreType.DMA((6,)),
                pltpu.SemaphoreType.DMA((2, 2)),
                pltpu.SemaphoreType.DMA((2, 2)),
                pltpu.SemaphoreType.DMA((2, n_col)),
                pltpu.SemaphoreType.DMA((2, n_col)),
                pltpu.SemaphoreType.DMA((2, n_row)),
                pltpu.SemaphoreType.DMA((2, n_row)),
                pltpu.SemaphoreType.DMA((n_row + n_col,)),
                pltpu.SemaphoreType.DMA((n_row + n_col,)),
            ],
            compiler_params=pltpu.CompilerParams(
                collective_id=0, has_side_effects=True, vmem_limit_bytes=60 * 1024 * 1024
            ),
        )(
            rhs, w, near_offsets.T, by_tile(v_factor),
            mix_col[0], mix_row[0], by_tile(u_factor),
        )

    both = ("row", "col")
    return jax.shard_map(
        body,
        mesh=mesh,
        in_specs=(
            P(None, both),
            P(both, None, None),
            P(both, None),
            P(both, None),
            P("row", "col", None, None),
            P("row", "col", None, None),
            P(both, None),
        ),
        out_specs=(P(None, both), P(None, both)),
        check_vma=False,
    )
```

time: 287 us -> 61 us (0.21); the launches traced: 282 us -> 60.8 us
  blocking collectives: 92.7 us -> 0 us
  local copies, waits for them, and re-layouts: 91.4 us -> 4.52 us
  Pallas kernels: 0 us -> 55.7 us
  starting transfers between devices: 41.1 us -> 0 us
  matrix products: 36.4 us -> 0 us
  other arithmetic: 19.3 us -> 0 us
    psum x12 -> x0, blocking collectives: 92.7 us -> none  [one_axis_at_a_time(): return functools.reduce(lax.psum, axes, x)]
    pallas_call x0 -> x1, Pallas kernels: none -> 55.7 us  [body(): pl.pallas_call(functools.partial(kernel, n_row, n_col), out_shape=[jax.Sh...]
    reshape x17 -> x0, local copies, waits for them, and re-layouts: 53.4 us -> none  [the longest x1 13 us: near_part(): blocks = near_blocks.reshape(leaves, blocks_per, LEAF, LEAF)]
    dot_general x10 -> x0, matrix products: 36.4 us -> none  [the longest x2 13.9 us: near_part(): jnp.einsum('slnu,lnvu->slv', picked, blocks, preferred_element_type=jnp.f...]
    all_to_all x4 -> x0, starting transfers between devices: 23.4 us -> none  [the longest x2 14.4 us: far_part(): lax.all_to_all(first, ROW, split_axis=0, concat_axis=0, tiled=True)]
    ppermute x4 -> x0, starting transfers between devices: 17.8 us -> none  [the longest x2 13.9 us: extended(): lax.ppermute(first, axis, [(b, a) for a, b in up])]
    transpose x4 -> x0, local copies, waits for them, and re-layouts: 10.4 us -> none  [the longest x2 5.23 us: near_part(): jnp.einsum('slnu,lnvu->slv', picked, blocks, preferred_element_type=jnp.f...]
    gather x2 -> x0, local copies, waits for them, and re-layouts: 8.87 us -> none  [near_part(): picked = padded[:, position, :]]
  transfers between devices with their start and end apart: 8 -> 0, of which waited for: 0 -> 0; matrix products, arithmetic and copies ran while one was open for 32% -> 0% of each run, Pallas kernels for 0% -> 0%
where the time goes in v1:
time: 61 us; the launch traced here: 60.8 us
  Pallas kernels  55.7 us (91%)
  local copies, waits for them, and re-layouts  4.52 us (7%)
  between operations  0.64 us (1%)
    pallas_call x1, Pallas kernels, body(): pl.pallas_call(functools.partial(kernel, n_row, n_col), out_shape=[jax.Sh...  55.7 us
    unnamed x2, local copies, waits for them, and re-layouts  4.52 us

profile of v1, /device:TPU:1, one launch (start us, length us, event | category | flops | bytes accessed | tf_op | source)
XLA Modules:
  0.0 60.8 jit_solution(8892376630942968667)
XLA Ops:
  0.6 55.7 %shard_map.86 = (f32[32,8192]{1,0:T(8,128)}, f32[32,8192]{1,0:T(8,128)}) custom-call(f32[32,8192]{1,0:T(8,128)} %r_hbm.1, bf16[16384,128]{1,0:T(8,128)(2,1)} %bitcast.18, s32[4,128]{1,0:T(4,128)} %bitcast.23, bf16[2048,128]{1,0:T(8,128)(2,1)} %bitcast.21, bf16[8,512,512]{2,1,0:T(8,128)(2,1)} %bitcast.19, bf16[16,256,256]{2,1,0:T(8,128)(2,1)} %bitcast.20, ...), custom_call_target="tpu_custom_call" | custom-call | tf_op jit(solution)/shard_map/pallas_call | solution.py:408
  56.3 2.3 %copy.12 = f32[32,8192]{1,0:T(8,128)} copy(f32[32,8192]{1,0:T(8,128)} %get-tuple-element.4) | data formatting | bytes 2097152
  58.6 2.3 %copy.13 = f32[32,8192]{1,0:T(8,128)} copy(f32[32,8192]{1,0:T(8,128)} %get-tuple-element.5) | data formatting | bytes 2097152

commit v2 on v1

--- a/solution.py
+++ b/solution.py
@@ -40,9 +40,9 @@
 
 def kernel(
     n_row, n_col,
-    r_hbm, w_hbm, off, v_hbm, mc_hbm, mr_hbm, u_hbm,
-    sol, res,
-    rv, bv, dv, wraw, wp, vraw, vq, uraw, uq, mc, mr, xlo, xhi,
+    r_hbm, w_hbm, off_hbm, v_hbm, mc_hbm, mr_hbm, u_hbm,
+    rv, bv, dv, coefs,
+    off, wraw, wp, vraw, vq, uraw, uq, mc, mr, xlo, xhi,
     hs, hr, zs, zr, zt, ts, tr, tt, sa, sb, g1, h1, g2, h2,
     load_sem, hs_sem, hr_sem, zs_sem, zr_sem, ts_sem, tr_sem, g_sem, h_sem,
 ):
@@ -50,7 +50,7 @@
     col = lax.axis_index("col")
     flat = row * n_col + col
     total = n_row * n_col
-    leaves = off.shape[1]
+    leaves = off_hbm.shape[1]
     lane = lane_index()
     low_half = lane < 64
 
@@ -65,6 +65,7 @@
     mc_load = loads(3, mc_hbm, mc)
     mr_load = loads(4, mr_hbm, mr)
     u_load = loads(5, u_hbm, uraw)
+    off_load = loads(6, off_hbm, off)
 
     def other_col(k):
         return lax.rem(col + k, n_col)
@@ -103,61 +104,68 @@
         group = lax.broadcasted_iota(jnp.int32, (16, 128), 1) // RANK
 
         def step(at, _):
-            sa[0] = vraw[pl.ds(pl.multiple_of(at * 128, 128), 128), :].astype(F32)
+            for k in range(2):
+                one(2 * at + k, k)
+            return 0
+
+        def one(at, k):
+            sa[k] = vraw[pl.ds(pl.multiple_of(at * 128, 128), 128), :].astype(F32)
             for leaf in range(8):
                 j = leaf % 4
-                part = sa[0, pl.ds(leaf, 16, stride=8), :]
+                part = sa[k, pl.ds(leaf, 16, stride=8), :]
                 for w in range(4):
                     turned = part if j == w else pltpu.roll(part, ((j - w) % 4) * RANK, 1)
-                    sb[2 * (leaf // 4) + j // 2, pl.ds((j % 2) * 64 + w, 16, stride=4), :] = jnp.where(
+                    sb[4 * k + 2 * (leaf // 4) + j // 2, pl.ds((j % 2) * 64 + w, 16, stride=4), :] = jnp.where(
                         group == j, turned, 0.0
                     )
             for q in range(4):
-                vq[pl.ds(pl.multiple_of(at * 512 + q * 128, 128), 128), :] = sb[q].astype(BF16)
-            return 0
-
-        lax.fori_loop(0, leaves // 8, step, 0)
+                vq[pl.ds(pl.multiple_of(at * 512 + q * 128, 128), 128), :] = sb[4 * k + q].astype(BF16)
+
+        lax.fori_loop(0, leaves // 16, step, 0)
 
     def expand_u():
         half = lax.broadcasted_iota(jnp.int32, (16, 128), 1) // LEAF
         nothing = jnp.zeros((64, 128), BF16)
 
         def step(at, _):
-            sa[0] = uraw[pl.ds(pl.multiple_of(at * 128, 128), 128), :].astype(F32)
+            for k in range(4):
+                one(4 * at + k, k)
+            return 0
+
+        def one(at, k):
+            sa[k] = uraw[pl.ds(pl.multiple_of(at * 128, 128), 128), :].astype(F32)
             for leaf in range(8):
                 q = leaf % 4
-                part = sa[0, pl.ds(leaf, 16, stride=8), :]
+                part = sa[k, pl.ds(leaf, 16, stride=8), :]
                 turned = pltpu.roll(part, 64, 1)
                 for w in range(2):
-                    sb[leaf // 4, pl.ds(q * RANK + w, 16, stride=2), :] = jnp.where(
+                    sb[2 * k + leaf // 4, pl.ds(q * RANK + w, 16, stride=2), :] = jnp.where(
                         half == q % 2, part if w == q % 2 else turned, 0.0
                     )
             for q in range(2):
                 base = pl.multiple_of(at * 256 + q * 128, 128)
-                uq[pl.ds(base, 64), 0:128] = sb[q, 0:64].astype(BF16)
+                uq[pl.ds(base, 64), 0:128] = sb[2 * k + q, 0:64].astype(BF16)
                 uq[pl.ds(base, 64), 128:256] = nothing
                 uq[pl.ds(base + 64, 64), 0:128] = nothing
-                uq[pl.ds(base + 64, 64), 128:256] = sb[q, 64:128].astype(BF16)
-            return 0
-
-        lax.fori_loop(0, leaves // 8, step, 0)
+                uq[pl.ds(base + 64, 64), 128:256] = sb[2 * k + q, 64:128].astype(BF16)
+
+        lax.fori_loop(0, leaves // 32, step, 0)
 
     def expand_w(first, last):
         half = lax.broadcasted_iota(jnp.int32, (32, 128), 1) < 64
 
         def step(at, _):
-            for k in range(4):
-                leaf = at * 4 + k
+            for k in range(8):
+                leaf = at * 8 + k
                 sa[k] = wraw[pl.ds(pl.multiple_of(leaf * 128, 128), 128), :].astype(F32)
-            for k in range(4):
-                leaf = at * 4 + k
+            for k in range(8):
                 for b in range(2):
                     one = sa[k, pl.ds(2 * b, 32, stride=4), :]
                     two = sa[k, pl.ds(2 * b + 1, 32, stride=4), :]
                     sb[k, pl.ds(64 * b, 32, stride=2), :] = jnp.where(half, one, pltpu.roll(two, 64, 1))
                     sb[k, pl.ds(64 * b + 1, 32, stride=2), :] = jnp.where(half, pltpu.roll(one, 64, 1), two)
-            for k in range(4):
-                base = pl.multiple_of((at * 4 + k) * 64, 64)
+            for k in range(8):
+                base = pl.multiple_of((at * 8 + k) * 64, 64)
                 wp[pl.ds(base, 64), 0:128] = sb[k, 0:64].astype(BF16)
                 wp[pl.ds(base, 64), 128:256] = sb[k, 64:128].astype(BF16)
             return 0
@@ -198,12 +206,12 @@
 
     def spread(src):
         def step(at, _):
-            for k in range(4):
-                pair = at * 4 + k
+            for k in range(8):
+                pair = at * 8 + k
                 put_leaves(HALO + 2 * pair, src[:, pl.ds(pl.multiple_of(pair * 128, 128), 128)])
             return 0
 
-        lax.fori_loop(0, leaves // 8, step, 0)
+        lax.fori_loop(0, leaves // 16, step, 0)
 
     def spread_edges(app):
         for side, inside in ((0, flat > 0), (1, flat < total - 1)):
@@ -215,8 +223,8 @@
 
     def near(dst, first, last):
         def step(at, _):
-            for k in range(2):
-                pair = at * 2 + k
+            for k in range(8):
+                pair = at * 8 + k
                 parts = []
                 for leaf in (2 * pair, 2 * pair + 1):
                     index = [leaf + HALO + off[b, leaf] for b in range(4)]
@@ -234,28 +242,37 @@
 
         lax.fori_loop(first, last, step, 0)
 
-    def mix_columns(app):
+    def columns_arrive(app):
         for k in range(1, n_col):
             source = other_col(k)
             arrived(zr.at[app, source], zs_sem.at[app, source], zr_sem.at[app, source])
+
+    def mix_columns(app):
         for half in range(2):
             for c in range(n_col // 4):
                 tiles = [zr[app, 4 * c + i, half].astype(F32) for i in range(4)]
                 for j, tile in enumerate(blocks_swapped(tiles)):
                     zt[4 * half + j, :, 128 * c : 128 * (c + 1)] = tile.astype(BF16)
-        for k in list(range(1, n_row)) + [0]:
-            j = other_row(k)
-            t = dot(zt[j], mc[j]).astype(BF16)
-            if k:
-                ts[app, j] = t
-                send(ts.at[app, j], tr.at[app, row], ts_sem.at[app, j], tr_sem.at[app, row], (j, col))
-            else:
-                tr[app, row] = t
-
-    def mix_rows(app):
+        order = list(range(1, n_row)) + [0]
+        for first in range(0, n_row, 4):
+            ks = order[first : first + 4]
+            made = [dot(zt[other_row(k)], mc[other_row(k)]).astype(BF16) for k in ks]
+            for k, t in zip(ks, made):
+                if k:
+                    ts[app, other_row(k)] = t
+                else:
+                    tr[app, row] = t
+            for k in ks:
+                j = other_row(k)
+                if k:
+                    send(ts.at[app, j], tr.at[app, row], ts_sem.at[app, j], tr_sem.at[app, row], (j, col))
+
+    def rows_arrive(app):
         for k in range(1, n_row):
             source = other_row(k)
             arrived(tr.at[app, source], ts_sem.at[app, source], tr_sem.at[app, source])
+
+    def mix_rows(app):
         for p in range(n_col // 4):
             for r in range(n_row // 4):
                 tiles = [tr[app, 4 * r + i, :, 128 * p : 128 * (p + 1)].astype(F32) for i in range(4)]
@@ -264,14 +281,13 @@
 
     def expand(dst, sums):
         def step(at, carry):
-            for k in range(2):
-                p = at * 2 + k
-                t = dot(tt[p], mr[p])
-                high = t.astype(BF16)
+            ts_ = [dot(tt[at * 8 + k], mr[at * 8 + k]).astype(BF16) for k in range(8)]
+            for k, t in enumerate(ts_):
                 for q in range(2):
-                    base = pl.multiple_of((2 * p + q) * 256, 256)
-                    weights = uq[pl.ds(pl.multiple_of((2 * p + q) * 128, 128), 128), :]
-                    far = dot(high[:, 128 * q : 128 * (q + 1)], weights)
+                    quad = (at * 8 + k) * 2 + q
+                    base = pl.multiple_of(quad * 256, 256)
+                    weights = uq[pl.ds(pl.multiple_of(quad * 128, 128), 128), :]
+                    far = dot(t[:, 128 * q : 128 * (q + 1)], weights)
                     for part in range(2):
                         lanes = pl.ds(pl.multiple_of(base + part * 128, 128), 128)
                         out = dst[:, lanes] + far[:, part * 128 : (part + 1) * 128]
@@ -282,7 +298,7 @@
             return carry
 
         zero = jnp.zeros((S, 128), F32)
-        return lax.fori_loop(0, n_col // 2, step, (zero, zero, zero) if sums else 0)
+        return lax.fori_loop(0, n_col // 8, step, (zero, zero, zero) if sums else 0)
 
     def early_sums():
         def step(at, carry):
@@ -297,102 +313,146 @@
 
     groups = [list(range(1, 6)), list(range(6, 11)), list(range(11, n_col)) + [0]]
 
-    v_load.wait()
-    expand_v()
-    r_load.wait()
-    pl.semaphore_wait(barrier, len(partners))
-    send_edges(0, rv)
-    for group in groups:
-        compress(0, rv, group)
-    spread(rv)
-    w_load.wait()
-    expand_w(0, leaves // 4)
-    spread_edges(0)
-    mc_load.wait()
-    mix_columns(0)
-    u_load.wait()
-    expand_u()
-    near(bv, 0, leaves // 4)
-    mr_load.wait()
-    mix_rows(0)
-    expand(bv, False)
-
-    send_edges(1, bv)
-    for group in groups:
-        compress(1, bv, group)
-    spread(bv)
-    rr, rb, bb = early_sums()
-    spread_edges(1)
-    near(dv, 0, leaves // 8)
-    mix_columns(1)
-    near(dv, leaves // 8, leaves // 4)
-    mix_rows(1)
-    rd, bd, dd = expand(dv, True)
-
-    small = lax.broadcasted_iota(jnp.int32, (8, 128), 1)
-    packed = jnp.zeros((8, 128), F32)
-    for q, products in enumerate((rr, rb, bb, rd, bd, dd)):
-        column = jnp.sum(products, axis=1, keepdims=True)
-        for g in range(S // 8):
-            packed = jnp.where(small == 8 * g + q, column[8 * g : 8 * (g + 1)], packed)
-    g1[...] = packed
-    h1[row] = packed
-    for k in range(1, n_row):
-        to = other_row(k)
-        send(g1, h1.at[row], g_sem.at[to], h_sem.at[row], (to, col))
-    for k in range(1, n_row):
-        source = other_row(k)
-        arrived(h1.at[source], g_sem.at[source], h_sem.at[source])
-    packed = h1[0]
-    for k in range(1, n_row):
-        packed = packed + h1[k]
-    g2[...] = packed
-    h2[col] = packed
-    for k in range(1, n_col):
-        to = other_col(k)
-        send(g2, h2.at[col], g_sem.at[n_row + to], h_sem.at[n_row + col], (row, to))
-    for k in range(1, n_col):
-        source = other_col(k)
-        arrived(h2.at[source], g_sem.at[n_row + source], h_sem.at[n_row + source])
-    packed = h2[0]
-    for k in range(1, n_col):
-        packed = packed + h2[k]
+    def at(name):
+        return jax.named_scope(name)
+
+    with at("load_v"):
+        v_load.wait()
+    with at("expand_v"):
+        expand_v()
+    with at("entry"):
+        r_load.wait()
+        pl.semaphore_wait(barrier, len(partners))
+    with at("z0"):
+        send_edges(0, rv)
+        for group in groups:
+            compress(0, rv, group)
+    with at("spread0"):
+        spread(rv)
+    with at("expand_w"):
+        w_load.wait()
+        expand_w(0, leaves // 8)
+    with at("edges0"):
+        spread_edges(0)
+    with at("waitcol0"):
+        mc_load.wait()
+        columns_arrive(0)
+    with at("mixcol0"):
+        mix_columns(0)
+    with at("expand_u"):
+        u_load.wait()
+        expand_u()
+    with at("near0"):
+        off_load.wait()
+        near(bv, 0, leaves // 16)
+    with at("waitrow0"):
+        mr_load.wait()
+        rows_arrive(0)
+    with at("swaprow0"):
+        mix_rows(0)
+    with at("expand0"):
+        expand(bv, False)
+    with at("z1"):
+        send_edges(1, bv)
+        for group in groups:
+            compress(1, bv, group)
+    with at("spread1"):
+        spread(bv)
+    with at("sums"):
+        rr, rb, bb = early_sums()
+    with at("edges1"):
+        spread_edges(1)
+    with at("near1a"):
+        near(dv, 0, leaves // 32)
+    with at("waitcol1"):
+        columns_arrive(1)
+    with at("mixcol1"):
+        mix_columns(1)
+    with at("near1b"):
+        near(dv, leaves // 32, leaves // 16)
+    with at("waitrow1"):
+        rows_arrive(1)
+    with at("swaprow1"):
+        mix_rows(1)
+    with at("expand1"):
+        rd, bd, dd = expand(dv, True)
+
+    with at("reduce"):
+        small = lax.broadcasted_iota(jnp.int32, (8, 128), 1)
+        packed = jnp.zeros((8, 128), F32)
+        for q, products in enumerate((rr, rb, bb, rd, bd, dd)):
+            column = jnp.sum(products, axis=1, keepdims=True)
+            for g in range(S // 8):
+                packed = jnp.where(small == 8 * g + q, column[8 * g : 8 * (g + 1)], packed)
+        g1[...] = packed
+        h1[row] = packed
+        for k in range(1, n_row):
+            to = other_row(k)
+            send(g1, h1.at[row], g_sem.at[to], h_sem.at[row], (to, col))
+        for k in range(1, n_row):
+            source = other_row(k)
+            arrived(h1.at[source], g_sem.at[source], h_sem.at[source])
+        packed = h1[0]
+        for k in range(1, n_row):
+            packed = packed + h1[k]
+        g2[...] = packed
+        h2[col] = packed
+        for k in range(1, n_col):
+            to = other_col(k)
+            send(g2, h2.at[col], g_sem.at[n_row + to], h_sem.at[n_row + col], (row, to))
+        for k in range(1, n_col):
+            source = other_col(k)
+            arrived(h2.at[source], g_sem.at[n_row + source], h_sem.at[n_row + source])
+        packed = h2[0]
+        for k in range(1, n_col):
+            packed = packed + h2[k]
 
     def of(q):
         return jnp.concatenate([packed[:, 8 * g + q : 8 * g + q + 1] for g in range(S // 8)], axis=0)
 
-    rr, rb, bb, rd, bd, dd = (of(q) for q in range(6))
-    inv = 1.0 / rr
-    shift = rb * inv
-    h21s = bb * inv - shift * shift
-    h21 = jnp.sqrt(h21s)
-    h11 = 1.0 + shift
-    h12 = (rd - shift * rb) * inv / h21
-    k22 = (bd - shift * bb - shift * rd + shift * shift * rb) * inv / h21s
-    size = (dd - 2.0 * shift * bd + shift * shift * bb) * inv / h21s
-    h32s = size - h12 * h12 - k22 * k22
-    h22 = 1.0 + k22
-    m11 = h11 * h11 + h21s
-    m12 = h11 * h12 + h21 * h22
-    m22 = h12 * h12 + h22 * h22 + h32s
-    det = m11 * m22 - m12 * m12
-    y1 = (m22 * h11 - m12 * h12) / det
-    y2 = (m11 * h12 - m12 * h11) / det / h21
-    wide = lambda x: jnp.broadcast_to(x, (S, 128))
-    sol_r, sol_b = wide(y1 - y2 * shift), wide(y2)
-    res_r, res_b = wide(1.0 - y1 + y2 * shift), wide(y1 + y2 - y2 * shift)
-
-    def finish(at, _):
-        for k in range(4):
-            lanes = pl.ds(pl.multiple_of((at * 4 + k) * 128, 128), 128)
+    with at("coefs"):
+        rr, rb, bb, rd, bd, dd = (of(q) for q in range(6))
+        inv = 1.0 / rr
+        shift = rb * inv
+        h21s = bb * inv - shift * shift
+        h21 = jnp.sqrt(h21s)
+        h11 = 1.0 + shift
+        h12 = (rd - shift * rb) * inv / h21
+        k22 = (bd - shift * bb - shift * rd + shift * shift * rb) * inv / h21s
+        size = (dd - 2.0 * shift * bd + shift * shift * bb) * inv / h21s
+        h32s = size - h12 * h12 - k22 * k22
+        h22 = 1.0 + k22
+        m11 = h11 * h11 + h21s
+        m12 = h11 * h12 + h21 * h22
+        m22 = h12 * h12 + h22 * h22 + h32s
+        det = m11 * m22 - m12 * m12
+        y1 = (m22 * h11 - m12 * h12) / det
+        y2 = (m11 * h12 - m12 * h11) / det / h21
+        for q, x in enumerate((y1 - y2 * shift, y2, 1.0 - y1 + y2 * shift, y1 + y2 - y2 * shift)):
+            coefs[q] = jnp.broadcast_to(x, (S, 128))
+
+    with at("drain"):
+        for copy in sends:
+            copy.wait_send()
+
+
+def finish(rv, bv, dv, coefs, sol_hbm, res_hbm, sol, res, sem):
+    sol_r, sol_b, res_r, res_b = (coefs[q] for q in range(4))
+    pieces = sem.shape[1]
+    width = rv.shape[1] // pieces
+    copies = []
+    for piece in range(pieces):
+        for at in range(piece * width, (piece + 1) * width, 128):
+            lanes = slice(at, at + 128)
             r, b, d = rv[:, lanes], bv[:, lanes], dv[:, lanes]
             sol[:, lanes] = sol_r * r + sol_b * b
             res[:, lanes] = res_r * r - res_b * b - sol_b * d
-        return 0
-
-    lax.fori_loop(0, leaves // 8, finish, 0)
-    for copy in sends:
-        copy.wait_send()
+        lanes = pl.ds(piece * width, width)
+        for k, (src, dst) in enumerate(((sol, sol_hbm), (res, res_hbm))):
+            copies.append(pltpu.make_async_copy(src.at[:, lanes], dst.at[:, lanes], sem.at[k, piece]))
+            copies[-1].start()
+    for copy in copies:
+        copy.wait()
 
 
 def solution(mesh):
@@ -405,13 +465,14 @@
         by_tile = lambda x: x.reshape(leaves // 8, 8, 16, 128).transpose(0, 2, 1, 3).reshape(leaves * 16, 128)
         any_spec = pl.BlockSpec(memory_space=pl.ANY)
         field = pltpu.VMEM((S, unknowns), F32)
-        return pl.pallas_call(
+        vmem_spec = pl.BlockSpec(memory_space=pltpu.VMEM)
+        parts = pl.pallas_call(
             functools.partial(kernel, n_row, n_col),
-            out_shape=[jax.ShapeDtypeStruct((S, unknowns), F32)] * 2,
-            in_specs=[any_spec, any_spec, pl.BlockSpec(memory_space=pltpu.SMEM)] + [any_spec] * 4,
-            out_specs=[pl.BlockSpec(memory_space=pltpu.VMEM)] * 2,
+            out_shape=[field, field, field, pltpu.VMEM((4, S, 128), F32)],
+            in_specs=[pl.BlockSpec(memory_space=pltpu.HBM)] * 7,
+            out_specs=[vmem_spec] * 4,
             scratch_shapes=[
-                field, field, field,
+                pltpu.SMEM((4, leaves), jnp.int32),
                 pltpu.VMEM((leaves * 128, 128), BF16),
                 pltpu.VMEM((leaves * 64, 256), BF16),
                 pltpu.VMEM((leaves * 16, 128), BF16),
@@ -430,13 +491,13 @@
                 pltpu.VMEM((2, n_row, S, n_col * RANK), BF16),
                 pltpu.VMEM((2, n_row, S, n_col * RANK), BF16),
                 pltpu.VMEM((n_col, S, n_row * RANK), BF16),
-                pltpu.VMEM((4, 128, 128), F32),
-                pltpu.VMEM((4, 128, 128), F32),
+                pltpu.VMEM((8, 128, 128), F32),
+                pltpu.VMEM((8, 128, 128), F32),
                 pltpu.VMEM((8, 128), F32),
                 pltpu.VMEM((n_row, 8, 128), F32),
                 pltpu.VMEM((8, 128), F32),
                 pltpu.VMEM((n_col, 8, 128), F32),
-                pltpu.SemaphoreType.DMA((6,)),
+                pltpu.SemaphoreType.DMA((7,)),
                 pltpu.SemaphoreType.DMA((2, 2)),
                 pltpu.SemaphoreType.DMA((2, 2)),
                 pltpu.SemaphoreType.DMA((2, n_col)),
@@ -447,12 +508,24 @@
                 pltpu.SemaphoreType.DMA((n_row + n_col,)),
             ],
             compiler_params=pltpu.CompilerParams(
-                collective_id=0, has_side_effects=True, vmem_limit_bytes=60 * 1024 * 1024
+                collective_id=0, has_side_effects=True, vmem_limit_bytes=54 * 1024 * 1024
             ),
         )(
             rhs, w, near_offsets.T, by_tile(v_factor),
             mix_col[0], mix_row[0], by_tile(u_factor),
         )
+        return pl.pallas_call(
+            finish,
+            out_shape=[jax.ShapeDtypeStruct((S, unknowns), F32)] * 2,
+            in_specs=[vmem_spec] * 4,
+            out_specs=[any_spec] * 2,
+            scratch_shapes=[
+                pltpu.VMEM((S, unknowns), F32),
+                pltpu.VMEM((S, unknowns), F32),
+                pltpu.SemaphoreType.DMA((2, 4)),
+            ],
+            compiler_params=pltpu.CompilerParams(vmem_limit_bytes=8 * 1024 * 1024),
+        )(*(pltpu.with_memory_space_constraint(x, pltpu.VMEM) for x in parts))
 
     both = ("row", "col")
     return jax.shard_map(

time: 61 us -> 47.2 us (0.77)
  Pallas kernels: 55.7 us -> 46.5 us
  local copies, waits for them, and re-layouts: 4.52 us -> 0 us
    pallas_call x1 -> x2, Pallas kernels: 55.7 us -> 46.5 us  [the longest x1 45.1 us: body(): pl.pallas_call(functools.partial(kernel, n_row, n_col), out_shape=[field,...]
    unnamed x2 -> x0, local copies, waits for them, and re-layouts: 4.52 us -> none
where the time goes in v2:
time: 47.2 us; the launch traced here: 47.1 us
  Pallas kernels  46.5 us (99%)
  between operations  0.64 us (1%)
    pallas_call x1, Pallas kernels, body(): pl.pallas_call(functools.partial(kernel, n_row, n_col), out_shape=[field,...  45.1 us
    pallas_call x1, Pallas kernels, body(): pl.pallas_call(finish, out_shape=[jax.ShapeDtypeStruct((S, unknowns), F32...  1.42 us

profile of v2, /device:TPU:1, one launch (start us, length us, event | category | flops | bytes accessed | tf_op | source)
XLA Modules:
  0.0 47.1 jit_solution(17301106629387828549)
XLA Ops:
  0.6 45.1 %shard_map.86 = (f32[32,8192]{1,0:T(8,128)S(1)}, f32[32,8192]{1,0:T(8,128)S(1)}, f32[32,8192]{1,0:T(8,128)S(1)}, f32[4,32,128]{2,1,0:T(8,128)S(1)}) custom-call(f32[32,8192]{1,0:T(8,128)} %r_hbm.1, bf16[16384,128]{1,0:T(8,128)(2,1)} %bitcast.18, s32[4,128]{1,0:T(4,128)} %bitcast.23, bf16[2048,128]{1,0:T(8,128)(2,1)} %bitcast.21, ...), custom_call_target="tpu_custom_call" | custom-call | tf_op jit(solution)/shard_map/pallas_call | solution.py:469
  45.7 1.4 %shard_map.87 = (f32[32,8192]{1,0:T(8,128)}, f32[32,8192]{1,0:T(8,128)}) custom-call(f32[32,8192]{1,0:T(8,128)S(1)} %get-tuple-element.6.rv, f32[32,8192]{1,0:T(8,128)S(1)} %get-tuple-element.7.bv, f32[32,8192]{1,0:T(8,128)S(1)} %get-tuple-element.8.dv, f32[4,32,128]{2,1,0:T(8,128)S(1)} %get-tuple-element.9.coefs), custom_call_target="tpu_custom_call" | custom-call | tf_op jit(solution)/shard_map/pallas_call | solution.py:517

commit v3 on v2

v3 whole, which is shorter than its diff:
```python
import functools

import jax
import jax.numpy as jnp
from jax import lax
from jax.experimental import pallas as pl
from jax.experimental.pallas import tpu as pltpu
from jax.sharding import PartitionSpec as P

S = 32
LEAF = 64
RANK = 32
HALO = 4
F32 = jnp.float32
BF16 = jnp.bfloat16
MESH = pl.DeviceIdType.MESH
NT = (((1,), (1,)), ((), ()))


def dot(a, b):
    return jnp.dot(a, b, preferred_element_type=F32)


def lane_index():
    return lax.broadcasted_iota(jnp.int32, (S, 128), 1)


def blocks_swapped(tiles):
    lane = lane_index()
    low_half = lane < 64
    low_quarter = lax.rem(lane, 64) < 32
    a, b, c, d = tiles
    turn = lambda x, by: pltpu.roll(x, by, 1)
    a, c = jnp.where(low_half, a, turn(c, 64)), jnp.where(low_half, turn(a, 64), c)
    b, d = jnp.where(low_half, b, turn(d, 64)), jnp.where(low_half, turn(b, 64), d)
    a, b = jnp.where(low_quarter, a, turn(b, 32)), jnp.where(low_quarter, turn(a, 96), b)
    c, d = jnp.where(low_quarter, c, turn(d, 32)), jnp.where(low_quarter, turn(c, 96), d)
    return a, b, c, d


def kernel(
    n_row, n_col,
    r_hbm, w_hbm, off_hbm, v_hbm, mc_hbm, mr_hbm, u_hbm,
    rv, bv, dv, coefs,
    off, wraw, wp, vraw, vq, uraw, uq, mc, mr, xd, turn,
    hs, hr, zs, zr, zt, ts, tr, tt, t2, sv, sa, sb, g1, h1, g2, h2,
    load_sem, sent, hr_sem, zr_sem, tr_sem, h_sem,
):
    row = lax.axis_index("row")
    col = lax.axis_index("col")
    flat = row * n_col + col
    total = n_row * n_col
    leaves = off_hbm.shape[1]
    lane = lane_index()
    low_half = lane < 64

    def loads(index, src, dst):
        copy = pltpu.make_async_copy(src, dst, load_sem.at[index])
        copy.start()
        return copy

    col_slow, col_fast, row_fast = lax.div(col, 4), lax.rem(col, 4), lax.rem(row, 4)
    home = lax.div(row, 4)
    away = 1 - home
    steps = [(z, y) for z in range(4) for y in range(4)]
    steps.sort(key=lambda d: -min(d[0], 4 - d[0]) - min(d[1], 4 - d[1]))
    order = [4 * lax.rem(col_slow + z, 4) + lax.rem(col_fast + y, 4) for z, y in steps]
    own = order[-1]
    inner = leaves // 2 - 16

    def at_half(half):
        return 0 if half is away else 1


    for group in range(4):
        for to in order[4 * group : 4 * (group + 1)]:
            rows = pl.ds(pl.multiple_of(to * 128, 128), 128)
            pltpu.make_async_copy(v_hbm.at[rows], vraw.at[rows], load_sem.at[5 + 2 * group]).start()
            lanes = pl.ds(pl.multiple_of(to * 512, 512), 512)
            pltpu.make_async_copy(r_hbm.at[:, lanes], rv.at[:, lanes], load_sem.at[6 + 2 * group]).start()
    off_load = loads(0, off_hbm, off)
    w_load = loads(1, w_hbm, wraw)

    def first_loads(group):
        pltpu.make_async_copy(v_hbm.at[0:512], vraw.at[0:512], load_sem.at[5 + 2 * group]).wait()
        pltpu.make_async_copy(r_hbm.at[:, 0:2048], rv.at[:, 0:2048], load_sem.at[6 + 2 * group]).wait()

    def other_col(k):
        return lax.rem(col + k, n_col)

    def other_row(k):
        return lax.rem(row + k, n_row)

    def at_flat(k):
        other = lax.rem(flat + k, total)
        return (lax.div(other, n_col), lax.rem(other, n_col))

    up, down = at_flat(1), at_flat(total - 1)
    barrier = pltpu.get_barrier_semaphore()
    partners = [(row, other_col(k)) for k in range(1, n_col)]
    partners += [(other_row(k), col) for k in range(1, n_row)] + [up, down]
    for partner in partners:
        pl.semaphore_signal(barrier, inc=1, device_id=partner, device_id_type=MESH)

    def send(src, dst, send_sem, recv_sem, device):
        pltpu.make_async_remote_copy(
            src_ref=src, dst_ref=dst, send_sem=send_sem, recv_sem=recv_sem,
            device_id=device, device_id_type=MESH,
        ).start()

    def arrived(all_of_them, recv_sem):
        pltpu.make_async_copy(all_of_them, all_of_them, recv_sem).wait()

    def set_turn():
        m = lax.broadcasted_iota(jnp.int32, (256, 256), 0)
        n = lax.broadcasted_iota(jnp.int32, (256, 256), 1)
        source = (n // 64) * 64 + 4 * lax.rem(n, 16) + lax.rem(n, 64) // 16
        turn[...] = jnp.where(m == source, 1.0, 0.0).astype(BF16)

    def expand_v(to, half):
        group = lax.broadcasted_iota(jnp.int32, (16, 128), 1) // RANK
        base = pl.multiple_of(to * 128, 128)
        pieces = []
        for j in range(4):
            part = sv[pl.ds(base + 4 * half + j, 16, stride=8), :].astype(BF16)
            for w in range(4):
                turned = part if j == w else pltpu.roll(part, ((j - w) % 4) * RANK, 1)
                pieces.append(jnp.where(group == j, turned, jnp.zeros_like(turned)))
        expanded = jnp.concatenate(pieces, axis=0)
        vq[pl.ds(pl.multiple_of((2 * to + half) * 256, 256), 256), :] = expanded
        return expanded

    def expand_u():
        half = lax.broadcasted_iota(jnp.int32, (16, 128), 1) // LEAF
        nothing = jnp.zeros((64, 128), BF16)

        def step(at, _):
            for k in range(8):
                one(8 * at + k, k)
            return 0

        def one(at, k):
            sa[k] = uraw[pl.ds(pl.multiple_of(at * 128, 128), 128), :].astype(F32)
            for leaf in range(8):
                q = leaf % 4
                part = sa[k, pl.ds(leaf, 16, stride=8), :]
                turned = pltpu.roll(part, 64, 1)
                for w in range(2):
                    sb[2 * k + leaf // 4, pl.ds(q * RANK + w, 16, stride=2), :] = jnp.where(
                        half == q % 2, part if w == q % 2 else turned, 0.0
                    )
            for q in range(2):
                base = pl.multiple_of(at * 256 + q * 128, 128)
                uq[pl.ds(base, 64), 0:128] = sb[2 * k + q, 0:64].astype(BF16)
                uq[pl.ds(base, 64), 128:256] = nothing
                uq[pl.ds(base + 64, 64), 0:128] = nothing
                uq[pl.ds(base + 64, 64), 128:256] = sb[2 * k + q, 64:128].astype(BF16)

        lax.fori_loop(0, leaves // 64, step, 0)

    def expand_w(first, last):
        half = lax.broadcasted_iota(jnp.int32, (32, 128), 1) < 64

        def step(at, _):
            for k in range(16):
                leaf = at * 16 + k
                sa[k] = wraw[pl.ds(pl.multiple_of(leaf * 128, 128), 128), :].astype(F32)
            for k in range(16):
                for b in range(2):
                    one = sa[k, pl.ds(2 * b, 32, stride=4), :]
                    two = sa[k, pl.ds(2 * b + 1, 32, stride=4), :]
                    sb[k, pl.ds(64 * b, 32, stride=2), :] = jnp.where(half, one, pltpu.roll(two, 64, 1))
                    sb[k, pl.ds(64 * b + 1, 32, stride=2), :] = jnp.where(half, pltpu.roll(one, 64, 1), two)
            for k in range(16):
                base = pl.multiple_of((at * 16 + k) * 64, 64)
                wp[pl.ds(base, 64), 0:128] = sb[k, 0:64].astype(BF16)
                wp[pl.ds(base, 64), 128:256] = sb[k, 64:128].astype(BF16)
            return 0

        lax.fori_loop(first, last, step, 0)

    def send_edges(app, src):
        hs[app, 0] = src[:, 0 : HALO * LEAF].astype(BF16)
        hs[app, 1] = src[:, (leaves - HALO) * LEAF : leaves * LEAF].astype(BF16)
        send(hs.at[app, 0], hr.at[app, 1], sent.at[0], hr_sem.at[app], down)
        send(hs.at[app, 1], hr.at[app, 0], sent.at[0], hr_sem.at[app], up)

    def turned_fields(values):
        x = jnp.concatenate([x.astype(BF16) for x in values], axis=0)
        x = dot(x, turn[...]).astype(BF16)
        return [x[S * k : S * (k + 1)] for k in range(len(values))]

    def compress(app, half, tos, fields, factors):
        made = [dot(x, v).astype(BF16) for x, v in zip(fields, factors)]
        for to, z in zip(tos, made):
            if to is own:
                zr[app, half, col] = z
            else:
                zs[app, half, to] = z
        for to in tos:
            if to is not own:
                send(
                    zs.at[app, half, to], zr.at[app, half, col],
                    sent.at[1], zr_sem.at[app, at_half(half)], (row, to),
                )

    def quad(to, half):
        return pl.ds(pl.multiple_of((2 * to + half) * 256, 256), 256)

    def grouped(size):
        return [(half, order[at : at + size]) for half in (away, home) for at in range(0, n_col, size)]

    def first_compress(ready, others):
        waiting = None
        for at, group in enumerate(grouped(4) + [None]):
            made = None
            if at == 4:
                others()
            if group is not None:
                half, tos = group
                if half is away:
                    first_loads(at)
                for to in tos:
                    if half is away:
                        rows = pl.ds(pl.multiple_of(to * 128, 128), 128)
                        sv[rows, :] = vraw[rows, :].astype(F32)
                factors = [expand_v(to, half) for to in tos]
                made = (half, tos, turned_fields([rv[:, quad(to, half)] for to in tos]), factors)
            if waiting is not None:
                ready()
                compress(0, *waiting)
            waiting = made

    def expand_and_compress(app, dst):
        added = turned = None
        for group in grouped(8) + [None, None]:
            next_added = next_turned = None
            if group is not None:
                next_added = (*group, far_added(dst, *group))
            if added is not None:
                half, tos, values = added
                next_turned = (half, tos, turned_fields(values), [vq[quad(to, half), :] for to in tos])
            if turned is not None:
                compress(app + 1, *turned)
            added, turned = next_added, next_turned

    def far_added(dst, half, tos):
        fars = [
            dot(t2[half, to], uq[pl.ds(pl.multiple_of((2 * to + half) * 128, 128), 128), :]) for to in tos
        ]
        outs = []
        for to, far in zip(tos, fars):
            lanes = quad(to, half)
            out = dst[:, lanes] + far
            dst[:, lanes] = out
            outs.append(out)
        return outs

    def put_leaves(at, x):
        turned = pltpu.roll(x, 64, 1)
        xd[at] = jnp.where(low_half, x, turned)
        xd[at + 1] = jnp.where(low_half, turned, x)

    def spread(src):
        def step(at, _):
            for k in range(32):
                pair = at * 32 + k
                put_leaves(HALO + 2 * pair, src[:, pl.ds(pl.multiple_of(pair * 128, 128), 128)].astype(BF16))
            return 0

        lax.fori_loop(0, leaves // 64, step, 0)

    def spread_edges(app):
        arrived(hr.at[app], hr_sem.at[app])
        for side, inside in ((0, flat > 0), (1, flat < total - 1)):
            for pair in range(HALO // 2):
                x = hr[app, side, :, pair * 128 : (pair + 1) * 128]
                x = jnp.where(inside, x, jnp.zeros_like(x))
                put_leaves(side * (HALO + leaves) + 2 * pair, x)

    def near_pairs(dst, pairs):
        for pair in pairs:
            parts = []
            for leaf in (2 * pair, 2 * pair + 1):
                index = [leaf + HALO + off[b, leaf] for b in range(4)]
                parts.append(
                    jnp.concatenate(
                        [
                            jnp.where(low_half, xd[index[0]], xd[index[1]]),
                            jnp.where(low_half, xd[index[2]], xd[index[3]]),
                        ],
                        axis=1,
                    )
                )
            lhs = jnp.concatenate(parts, axis=0)
            rows = pl.ds(pair * 128 if isinstance(pair, int) else pl.multiple_of(pair * 128, 128), 128)
            out = lax.dot_general(lhs, wp[rows, :], NT, preferred_element_type=F32)
            dst[:, rows] = jnp.where(low_half, out[:S], out[S:])

    def near(dst, first, count):
        def step(at, _):
            near_pairs(dst, [first + at * 16 + k for k in range(16)])
            return 0

        lax.fori_loop(0, count // 16, step, 0)

    def near_edges(dst):
        near_pairs(dst, list(range(8)) + [leaves // 2 - 8 + j for j in range(8)])

    def columns(app, half):
        arrived(zr.at[app, 0, pl.ds(0, n_col - 1)], zr_sem.at[app, at_half(half)])
        for c in range(4):
            tiles = [zr[app, half, 4 * c + i] for i in range(4)]
            for j, tile in enumerate(blocks_swapped(tiles)):
                zt[4 * half + j, c] = tile

    def mix_columns(app, half):
        to_rows = [4 * half + lax.rem(row_fast + k, 4) for k in (1, 2, 3, 0)]
        made = []
        for j in to_rows:
            z = jnp.concatenate([zt[j, c] for c in range(4)], axis=1)
            made.append(dot(z, mc[j]).astype(BF16))
        for at, (j, t) in enumerate(zip(to_rows, made)):
            stays = half is home and at == 3
            for p in range(4):
                if stays:
                    tr[app, row, p] = t[:, 128 * p : 128 * (p + 1)]
                else:
                    ts[app, j, p] = t[:, 128 * p : 128 * (p + 1)]
        for at, j in enumerate(to_rows):
            if not (half is home and at == 3):
                send(
                    ts.at[app, j], tr.at[app, row],
                    sent.at[2], tr_sem.at[app, at_half(half)], (j, col),
                )

    def rows(app, half):
        arrived(tr.at[app, pl.ds(0, 4 if half is away else 3)], tr_sem.at[app, at_half(half)])
        for p in range(4):
            tiles = [tr[app, 4 * half + i, p] for i in range(4)]
            for j, tile in enumerate(blocks_swapped(tiles)):
                tt[4 * p + j, half] = tile

    def mix_rows(app):
        for at in range(0, n_col, 8):
            made = [
                dot(jnp.concatenate([tt[p, 0], tt[p, 1]], axis=1), mr[p]).astype(BF16) for p in range(at, at + 8)
            ]
            for p, t in zip(range(at, at + 8), made):
                t2[0, p] = t[:, 0:128]
                t2[1, p] = t[:, 128:256]

    def last_expand(dst):
        zero = jnp.zeros((S, 128), F32)
        rd, bd, dd = zero, zero, zero
        for at in range(0, 2 * n_col, 8):
            fars = [dot(t2[k % 2, k // 2], uq[128 * k : 128 * (k + 1), :]) for k in range(at, at + 8)]
            for k, far in zip(range(at, at + 8), fars):
                for part in range(2):
                    lanes = slice(256 * k + 128 * part, 256 * k + 128 * (part + 1))
                    out = dst[:, lanes] + far[:, 128 * part : 128 * (part + 1)]
                    dst[:, lanes] = out
                    rd, bd, dd = rd + rv[:, lanes] * out, bd + bv[:, lanes] * out, dd + out * out
        return rd, bd, dd

    def placed(packed, qs, sums):
        small = lax.broadcasted_iota(jnp.int32, (8, 128), 1)
        for q, products in zip(qs, sums):
            column = jnp.sum(products, axis=1, keepdims=True)
            for g in range(S // 8):
                packed = jnp.where(small == 8 * g + q, column[8 * g : 8 * (g + 1)], packed)
        return packed

    def early_sums():
        def step(at, carry):
            for k in range(16):
                lanes = pl.ds(pl.multiple_of((at * 16 + k) * 128, 128), 128)
                rx, bx = rv[:, lanes], bv[:, lanes]
                carry = (carry[0] + rx * rx, carry[1] + rx * bx, carry[2] + bx * bx)
            return carry

        zero = jnp.zeros((S, 128), F32)
        return lax.fori_loop(0, leaves // 32, step, (zero, zero, zero))

    def at(name):
        return jax.named_scope(name)

    set_turn()
    met = []

    def meet():
        if not met:
            pl.semaphore_wait(barrier, len(partners))
            met.append(True)

    later = []

    def others():
        for at, (src, dst) in enumerate(((mc_hbm, mc), (u_hbm, uraw), (mr_hbm, mr))):
            later.append(loads(2 + at, src, dst))

    with at("z0"):
        first_compress(meet, others)
        mc_load, u_load, mr_load = later
        send_edges(0, rv)
    with at("spread0"):
        spread(rv)
    with at("expand_w"):
        w_load.wait()
        expand_w(0, leaves // 16)
    mc_load.wait()
    with at("colA0"):
        columns(0, away)
    with at("mixA0"):
        mix_columns(0, away)
    with at("colB0"):
        columns(0, home)
    with at("mixB0"):
        mix_columns(0, home)
    with at("expand_u"):
        u_load.wait()
        expand_u()
    with at("near0"):
        off_load.wait()
        near(bv, 8, inner)
    with at("edges0"):
        spread_edges(0)
        near_edges(bv)
    with at("rowA0"):
        rows(0, away)
    with at("rowB0"):
        rows(0, home)
    with at("mixrow0"):
        mr_load.wait()
        mix_rows(0)
    with at("expz0"):
        expand_and_compress(0, bv)
        send_edges(1, bv)
    with at("spread1"):
        spread(bv)
    with at("sums"):
        packed = placed(jnp.zeros((8, 128), F32), (0, 1, 2), early_sums())
    with at("near1a"):
        near(dv, 8, 16)
    with at("colA1"):
        columns(1, away)
    with at("mixA1"):
        mix_columns(1, away)
    with at("colB1"):
        columns(1, home)
    with at("mixB1"):
        mix_columns(1, home)
    with at("near1b"):
        near(dv, 24, inner - 16)
    with at("edges1"):
        spread_edges(1)
        near_edges(dv)
    with at("rowA1"):
        rows(1, away)
    with at("rowB1"):
        rows(1, home)
    with at("mixrow1"):
        mix_rows(1)
    with at("expand1"):
        rd, bd, dd = last_expand(dv)

    with at("reduce"):
        packed = placed(packed, (3, 4, 5), (rd, bd, dd))
        g1[...] = packed
        h1[row] = packed
        for k in range(1, n_row):
            to = other_row(k)
            send(g1, h1.at[row], sent.at[3], h_sem.at[0], (to, col))
        arrived(h1.at[pl.ds(0, n_row - 1)], h_sem.at[0])
        packed = h1[0]
        for k in range(1, n_row):
            packed = packed + h1[k]
        g2[...] = packed
        h2[col] = packed
        for k in range(1, n_col):
            to = other_col(k)
            send(g2, h2.at[col], sent.at[4], h_sem.at[1], (row, to))
        arrived(h2.at[pl.ds(0, n_col - 1)], h_sem.at[1])
        packed = h2[0]
        for k in range(1, n_col):
            packed = packed + h2[k]

    with at("coefs"):
        rr, rb, bb, rd, bd, dd = (packed if q == 0 else pltpu.roll(packed, 128 - q, 1) for q in range(6))
        inv = 1.0 / rr
        shift = rb * inv
        h21s = bb * inv - shift * shift
        inv_h21s = 1.0 / h21s
        h21 = jnp.sqrt(h21s)
        inv_h21 = h21 * inv_h21s
        h11 = 1.0 + shift
        h12 = (rd - shift * rb) * (inv * inv_h21)
        k22 = (bd - shift * (bb + rd - shift * rb)) * (inv * inv_h21s)
        size = (dd - shift * (2.0 * bd - shift * bb)) * (inv * inv_h21s)
        h32s = size - h12 * h12 - k22 * k22
        h22 = 1.0 + k22
        m11 = h11 * h11 + h21s
        m12 = h11 * h12 + h21 * h22
        m22 = h12 * h12 + h22 * h22 + h32s
        inv_det = 1.0 / (m11 * m22 - m12 * m12)
        y1 = (m22 * h11 - m12 * h12) * inv_det
        y2 = (m11 * h12 - m12 * h11) * inv_det * inv_h21
        for q, x in enumerate((y1 - y2 * shift, y2, 1.0 - y1 + y2 * shift, y1 + y2 - y2 * shift)):
            for g in range(S // 8):
                coefs[q, 8 * g : 8 * (g + 1)] = jnp.broadcast_to(x[:, 8 * g : 8 * g + 1], (8, 128))

    with at("drain"):
        arrived(hs, sent.at[0])
        arrived(zs.at[:, :, pl.ds(0, n_col - 1)], sent.at[1])
        arrived(ts.at[:, pl.ds(0, n_row - 1)], sent.at[2])
        arrived(h1.at[pl.ds(0, n_row - 1)], sent.at[3])
        arrived(h2.at[pl.ds(0, n_col - 1)], sent.at[4])


def finish(rv, bv, dv, coefs, sol_hbm, res_hbm, sol, res, sem):
    sol_r, sol_b, res_r, res_b = (coefs[q] for q in range(4))
    pieces = sem.shape[1]
    width = rv.shape[1] // pieces
    copies = []
    for piece in range(pieces):
        for at in range(piece * width, (piece + 1) * width, 128):
            lanes = slice(at, at + 128)
            r, b, d = rv[:, lanes], bv[:, lanes], dv[:, lanes]
            sol[:, lanes] = sol_r * r + sol_b * b
            res[:, lanes] = res_r * r - res_b * b - sol_b * d
        lanes = pl.ds(piece * width, width)
        for k, (src, dst) in enumerate(((sol, sol_hbm), (res, res_hbm))):
            copies.append(pltpu.make_async_copy(src.at[:, lanes], dst.at[:, lanes], sem.at[k, piece]))
            copies[-1].start()
    for copy in copies:
        copy.wait()


def solution(mesh):
    n_row, n_col = mesh.shape["row"], mesh.shape["col"]

    def body(rhs, near_blocks, near_offsets, v_factor, mix_col, mix_row, u_factor):
        leaves = near_offsets.shape[0]
        unknowns = leaves * LEAF
        w = near_blocks.reshape(leaves, 4, 32, 128).transpose(0, 2, 1, 3).reshape(leaves * 128, 128)
        by_tile = lambda x: x.reshape(leaves // 8, 8, 16, 128).transpose(0, 2, 1, 3).reshape(leaves * 16, 128)
        any_spec = pl.BlockSpec(memory_space=pl.ANY)
        field = pltpu.VMEM((S, unknowns), F32)
        vmem_spec = pl.BlockSpec(memory_space=pltpu.VMEM)
        parts = pl.pallas_call(
            functools.partial(kernel, n_row, n_col),
            out_shape=[field, field, field, pltpu.VMEM((4, S, 128), F32)],
            in_specs=[pl.BlockSpec(memory_space=pltpu.HBM)] * 7,
            out_specs=[vmem_spec] * 4,
            scratch_shapes=[
                pltpu.SMEM((4, leaves), jnp.int32),
                pltpu.VMEM((leaves * 128, 128), BF16),
                pltpu.VMEM((leaves * 64, 256), BF16),
                pltpu.VMEM((leaves * 16, 128), BF16),
                pltpu.VMEM((leaves * 64, 128), BF16),
                pltpu.VMEM((leaves * 16, 128), BF16),
                pltpu.VMEM((leaves * 32, 256), BF16),
                pltpu.VMEM(mix_col.shape[1:], BF16),
                pltpu.VMEM(mix_row.shape[1:], BF16),
                pltpu.VMEM((leaves + 2 * HALO, S, 128), BF16),
                pltpu.VMEM((256, 256), BF16),
                pltpu.VMEM((2, 2, S, HALO * LEAF), BF16),
                pltpu.VMEM((2, 2, S, HALO * LEAF), BF16),
                pltpu.VMEM((2, 2, n_col, S, 128), BF16),
                pltpu.VMEM((2, 2, n_col, S, 128), BF16),
                pltpu.VMEM((n_row, 4, S, 128), BF16),
                pltpu.VMEM((2, n_row, 4, S, 128), BF16),
                pltpu.VMEM((2, n_row, 4, S, 128), BF16),
                pltpu.VMEM((n_col, 2, S, 128), BF16),
                pltpu.VMEM((2, n_col, S, 128), BF16),
                pltpu.VMEM((leaves * 16, 128), F32),
                pltpu.VMEM((16, 128, 128), F32),
                pltpu.VMEM((16, 128, 128), F32),
                pltpu.VMEM((8, 128), F32),
                pltpu.VMEM((n_row, 8, 128), F32),
                pltpu.VMEM((8, 128), F32),
                pltpu.VMEM((n_col, 8, 128), F32),
                pltpu.SemaphoreType.DMA((5 + 2 * 4,)),
                pltpu.SemaphoreType.DMA((5,)),
                pltpu.SemaphoreType.DMA((2,)),
                pltpu.SemaphoreType.DMA((2, 2)),
                pltpu.SemaphoreType.DMA((2, 2)),
                pltpu.SemaphoreType.DMA((2,)),
            ],
            compiler_params=pltpu.CompilerParams(
                collective_id=0, has_side_effects=True, vmem_limit_bytes=54 * 1024 * 1024
            ),
        )(
            rhs, w, near_offsets.T, by_tile(v_factor),
            mix_col[0], mix_row[0], by_tile(u_factor),
        )
        return pl.pallas_call(
            finish,
            out_shape=[jax.ShapeDtypeStruct((S, unknowns), F32)] * 2,
            in_specs=[vmem_spec] * 4,
            out_specs=[any_spec] * 2,
            scratch_shapes=[
                pltpu.VMEM((S, unknowns), F32),
                pltpu.VMEM((S, unknowns), F32),
                pltpu.SemaphoreType.DMA((2, 4)),
            ],
            compiler_params=pltpu.CompilerParams(vmem_limit_bytes=8 * 1024 * 1024),
        )(*(pltpu.with_memory_space_constraint(x, pltpu.VMEM) for x in parts))

    both = ("row", "col")
    return jax.shard_map(
        body,
        mesh=mesh,
        in_specs=(
            P(None, both),
            P(both, None, None),
            P(both, None),
            P(both, None),
            P("row", "col", None, None),
            P("row", "col", None, None),
            P(both, None),
        ),
        out_specs=(P(None, both), P(None, both)),
        check_vma=False,
    )
```

time: 47.2 us -> 42.2 us (0.89)
  Pallas kernels: 46.5 us -> 41.5 us
    pallas_call x1, Pallas kernels: 45.1 us -> 40.1 us  [body(): pl.pallas_call(functools.partial(kernel, n_row, n_col), out_shape=[field,...]
where the time goes in v3:
time: 42.2 us; the launch traced here: 42.1 us
  Pallas kernels  41.5 us (98%)
  between operations  0.64 us (2%)
    pallas_call x1, Pallas kernels, body(): pl.pallas_call(functools.partial(kernel, n_row, n_col), out_shape=[field,...  40.1 us
    pallas_call x1, Pallas kernels, body(): pl.pallas_call(finish, out_shape=[jax.ShapeDtypeStruct((S, unknowns), F32...  1.42 us

profile of v3, /device:TPU:1, one launch (start us, length us, event | category | flops | bytes accessed | tf_op | source)
XLA Modules:
  0.0 42.1 jit_solution(16993468884507630140)
XLA Ops:
  0.6 40.1 %shard_map.86 = (f32[32,8192]{1,0:T(8,128)S(1)}, f32[32,8192]{1,0:T(8,128)S(1)}, f32[32,8192]{1,0:T(8,128)S(1)}, f32[4,32,128]{2,1,0:T(8,128)S(1)}) custom-call(f32[32,8192]{1,0:T(8,128)} %r_hbm.1, bf16[16384,128]{1,0:T(8,128)(2,1)} %bitcast.18, s32[4,128]{1,0:T(4,128)} %bitcast.23, bf16[2048,128]{1,0:T(8,128)(2,1)} %bitcast.21, ...), custom_call_target="tpu_custom_call" | custom-call | tf_op jit(solution)/shard_map/pallas_call | solution.py:550
  40.7 1.4 %shard_map.87 = (f32[32,8192]{1,0:T(8,128)}, f32[32,8192]{1,0:T(8,128)}) custom-call(f32[32,8192]{1,0:T(8,128)S(1)} %get-tuple-element.6.rv, f32[32,8192]{1,0:T(8,128)S(1)} %get-tuple-element.7.bv, f32[32,8192]{1,0:T(8,128)S(1)} %get-tuple-element.8.dv, f32[4,32,128]{2,1,0:T(8,128)S(1)} %get-tuple-element.9.coefs), custom_call_target="tpu_custom_call" | custom-call | tf_op jit(solution)/shard_map/pallas_call | solution.py:597

commit v4 on v3

--- a/solution.py
+++ b/solution.py
@@ -43,7 +43,7 @@
     r_hbm, w_hbm, off_hbm, v_hbm, mc_hbm, mr_hbm, u_hbm,
     rv, bv, dv, coefs,
     off, wraw, wp, vraw, vq, uraw, uq, mc, mr, xd, turn,
-    hs, hr, zs, zr, zt, ts, tr, tt, t2, sv, sa, sb, g1, h1, g2, h2,
+    hs, hr, zs, zr, zt, ts, tr, tt, tp, t2, sv, sa, sb, g1, h1, g2, h2,
     load_sem, sent, hr_sem, zr_sem, tr_sem, h_sem,
 ):
     row = lax.axis_index("row")
@@ -60,8 +60,12 @@
         return copy
 
     col_slow, col_fast, row_fast = lax.div(col, 4), lax.rem(col, 4), lax.rem(row, 4)
-    home = lax.div(row, 4)
+    home = lax.rem(lax.div(row, 2), 2)
     away = 1 - home
+
+    def slot_of(half, i):
+        return 2 * half + (i % 2) + 4 * (i // 2)
+
     steps = [(z, y) for z in range(4) for y in range(4)]
     steps.sort(key=lambda d: -min(d[0], 4 - d[0]) - min(d[1], 4 - d[1]))
     order = [4 * lax.rem(col_slow + z, 4) + lax.rem(col_fast + y, 4) for z, y in steps]
@@ -69,13 +73,14 @@
     inner = leaves // 2 - 16
 
     def at_half(half):
-        return 0 if half is away else 1
-
+        return 0 if half is home else 1
 
     for group in range(4):
-        for to in order[4 * group : 4 * (group + 1)]:
+        for k in range(4 * group, 4 * (group + 1)):
+            to = order[k]
             rows = pl.ds(pl.multiple_of(to * 128, 128), 128)
-            pltpu.make_async_copy(v_hbm.at[rows], vraw.at[rows], load_sem.at[5 + 2 * group]).start()
+            place = vraw.at[pl.ds(128 * k, 128)]
+            pltpu.make_async_copy(v_hbm.at[rows], place, load_sem.at[5 + 2 * group]).start()
             lanes = pl.ds(pl.multiple_of(to * 512, 512), 512)
             pltpu.make_async_copy(r_hbm.at[:, lanes], rv.at[:, lanes], load_sem.at[6 + 2 * group]).start()
     off_load = loads(0, off_hbm, off)
@@ -117,18 +122,15 @@
         source = (n // 64) * 64 + 4 * lax.rem(n, 16) + lax.rem(n, 64) // 16
         turn[...] = jnp.where(m == source, 1.0, 0.0).astype(BF16)
 
-    def expand_v(to, half):
+    def expand_v(k, half):
         group = lax.broadcasted_iota(jnp.int32, (16, 128), 1) // RANK
-        base = pl.multiple_of(to * 128, 128)
         pieces = []
         for j in range(4):
-            part = sv[pl.ds(base + 4 * half + j, 16, stride=8), :].astype(BF16)
+            part = sv[k, pl.ds(slot_of(half, j), 16, stride=8), :].astype(BF16)
             for w in range(4):
                 turned = part if j == w else pltpu.roll(part, ((j - w) % 4) * RANK, 1)
                 pieces.append(jnp.where(group == j, turned, jnp.zeros_like(turned)))
-        expanded = jnp.concatenate(pieces, axis=0)
-        vq[pl.ds(pl.multiple_of((2 * to + half) * 256, 256), 256), :] = expanded
-        return expanded
+        vq[at_half(half), k] = jnp.concatenate(pieces, axis=0)
 
     def expand_u():
         half = lax.broadcasted_iota(jnp.int32, (16, 128), 1) // LEAF
@@ -142,11 +144,11 @@
         def one(at, k):
             sa[k] = uraw[pl.ds(pl.multiple_of(at * 128, 128), 128), :].astype(F32)
             for leaf in range(8):
-                q = leaf % 4
+                half_at, q = (leaf // 2) % 2, leaf % 2 + 2 * (leaf // 4)
                 part = sa[k, pl.ds(leaf, 16, stride=8), :]
                 turned = pltpu.roll(part, 64, 1)
                 for w in range(2):
-                    sb[2 * k + leaf // 4, pl.ds(q * RANK + w, 16, stride=2), :] = jnp.where(
+                    sb[2 * k + half_at, pl.ds(q * RANK + w, 16, stride=2), :] = jnp.where(
                         half == q % 2, part if w == q % 2 else turned, 0.0
                     )
             for q in range(2):
@@ -185,75 +187,60 @@
         send(hs.at[app, 0], hr.at[app, 1], sent.at[0], hr_sem.at[app], down)
         send(hs.at[app, 1], hr.at[app, 0], sent.at[0], hr_sem.at[app], up)
 
+    def field(src, to, half):
+        return jnp.concatenate([src[:, lanes] for lanes in tiles_of(to, half)], axis=1)
+
     def turned_fields(values):
         x = jnp.concatenate([x.astype(BF16) for x in values], axis=0)
         x = dot(x, turn[...]).astype(BF16)
         return [x[S * k : S * (k + 1)] for k in range(len(values))]
 
-    def compress(app, half, tos, fields, factors):
-        made = [dot(x, v).astype(BF16) for x, v in zip(fields, factors)]
-        for to, z in zip(tos, made):
-            if to is own:
+    def compress(app, half, ks, fields):
+        h = at_half(half)
+        made = [dot(x, vq[h, k]).astype(BF16) for k, x in zip(ks, fields)]
+        for k, z in zip(ks, made):
+            if k == n_col - 1:
                 zr[app, half, col] = z
             else:
-                zs[app, half, to] = z
-        for to in tos:
-            if to is not own:
-                send(
-                    zs.at[app, half, to], zr.at[app, half, col],
-                    sent.at[1], zr_sem.at[app, at_half(half)], (row, to),
-                )
-
-    def quad(to, half):
-        return pl.ds(pl.multiple_of((2 * to + half) * 256, 256), 256)
-
-    def grouped(size):
-        return [(half, order[at : at + size]) for half in (away, home) for at in range(0, n_col, size)]
+                zs[app, h, k] = z
+        for k in ks:
+            if k < n_col - 1:
+                send(zs.at[app, h, k], zr.at[app, half, col], sent.at[1], zr_sem.at[app, h], (row, order[k]))
+
+    def tiles_of(to, half):
+        return [pl.ds(pl.multiple_of(to * 512 + half * 128 + part * 256, 128), 128) for part in range(2)]
 
     def first_compress(ready, others):
-        waiting = None
-        for at, group in enumerate(grouped(4) + [None]):
-            made = None
-            if at == 4:
+        ks = list(range(n_col))
+        for half in (home, away):
+            if half is home:
+                for group in range(4):
+                    first_loads(group)
+                    for k in range(4 * group, 4 * group + 4):
+                        sv[k] = vraw[128 * k : 128 * (k + 1), :].astype(F32)
+            for k in ks:
+                expand_v(k, half)
+            fields = turned_fields([field(rv, to, half) for to in order])
+            if half is home:
+                ready()
+            compress(0, half, ks, fields)
+            if half is home:
                 others()
-            if group is not None:
-                half, tos = group
-                if half is away:
-                    first_loads(at)
-                for to in tos:
-                    if half is away:
-                        rows = pl.ds(pl.multiple_of(to * 128, 128), 128)
-                        sv[rows, :] = vraw[rows, :].astype(F32)
-                factors = [expand_v(to, half) for to in tos]
-                made = (half, tos, turned_fields([rv[:, quad(to, half)] for to in tos]), factors)
-            if waiting is not None:
-                ready()
-                compress(0, *waiting)
-            waiting = made
 
     def expand_and_compress(app, dst):
-        added = turned = None
-        for group in grouped(8) + [None, None]:
-            next_added = next_turned = None
-            if group is not None:
-                next_added = (*group, far_added(dst, *group))
-            if added is not None:
-                half, tos, values = added
-                next_turned = (half, tos, turned_fields(values), [vq[quad(to, half), :] for to in tos])
-            if turned is not None:
-                compress(app + 1, *turned)
-            added, turned = next_added, next_turned
+        for half in (home, away):
+            fields = turned_fields(far_added(dst, half, order))
+            compress(app + 1, half, list(range(n_col)), fields)
 
     def far_added(dst, half, tos):
         fars = [
             dot(t2[half, to], uq[pl.ds(pl.multiple_of((2 * to + half) * 128, 128), 128), :]) for to in tos
         ]
-        outs = []
-        for to, far in zip(tos, fars):
-            lanes = quad(to, half)
-            out = dst[:, lanes] + far
-            dst[:, lanes] = out
-            outs.append(out)
+        old = [field(dst, to, half) for to in tos]
+        outs = [x + far for x, far in zip(old, fars)]
+        for to, out in zip(tos, outs):
+            for part, lanes in enumerate(tiles_of(to, half)):
+                dst[:, lanes] = out[:, 128 * part : 128 * (part + 1)]
         return outs
 
     def put_leaves(at, x):
@@ -312,10 +299,10 @@
         for c in range(4):
             tiles = [zr[app, half, 4 * c + i] for i in range(4)]
             for j, tile in enumerate(blocks_swapped(tiles)):
-                zt[4 * half + j, c] = tile
+                zt[slot_of(half, j), c] = tile
 
     def mix_columns(app, half):
-        to_rows = [4 * half + lax.rem(row_fast + k, 4) for k in (1, 2, 3, 0)]
+        to_rows = [2 * half + lax.rem(lax.rem(row, 2) + k, 2) + 4 * lax.rem(lax.div(row, 4) + m, 2) for m, k in ((1, 0), (1, 1), (0, 1), (0, 0))]
         made = []
         for j in to_rows:
             z = jnp.concatenate([zt[j, c] for c in range(4)], axis=1)
@@ -327,28 +314,32 @@
                     tr[app, row, p] = t[:, 128 * p : 128 * (p + 1)]
                 else:
                     ts[app, j, p] = t[:, 128 * p : 128 * (p + 1)]
-        for at, j in enumerate(to_rows):
-            if not (half is home and at == 3):
-                send(
-                    ts.at[app, j], tr.at[app, row],
-                    sent.at[2], tr_sem.at[app, at_half(half)], (j, col),
-                )
+            if not stays:
+                send(ts.at[app, j], tr.at[app, row], sent.at[2], tr_sem.at[app, at_half(half)], (j, col))
 
     def rows(app, half):
         arrived(tr.at[app, pl.ds(0, 4 if half is away else 3)], tr_sem.at[app, at_half(half)])
         for p in range(4):
-            tiles = [tr[app, 4 * half + i, p] for i in range(4)]
+            tiles = [tr[app, slot_of(half, i), p] for i in range(4)]
             for j, tile in enumerate(blocks_swapped(tiles)):
                 tt[4 * p + j, half] = tile
 
-    def mix_rows(app):
+    def part_of_rows(p, half):
+        weights = [mr[p, pl.ds(pl.multiple_of(64 * half + 128 * i, 64), 64), :] for i in range(2)]
+        return dot(tt[p, half], jnp.concatenate(weights, axis=0))
+
+    def mix_rows_first(half):
         for at in range(0, n_col, 8):
-            made = [
-                dot(jnp.concatenate([tt[p, 0], tt[p, 1]], axis=1), mr[p]).astype(BF16) for p in range(at, at + 8)
-            ]
+            for p in range(at, at + 8):
+                tp[p] = part_of_rows(p, half)
+
+    def mix_rows(half):
+        for at in range(0, n_col, 8):
+            made = [(tp[p] + part_of_rows(p, half)).astype(BF16) for p in range(at, at + 8)]
             for p, t in zip(range(at, at + 8), made):
-                t2[0, p] = t[:, 0:128]
-                t2[1, p] = t[:, 128:256]
+                one, two = t[:, 0:128], t[:, 128:256]
+                t2[0, p] = jnp.where(low_half, one, pltpu.roll(two, 64, 1))
+                t2[1, p] = jnp.where(low_half, pltpu.roll(one, 64, 1), two)
 
     def last_expand(dst):
         zero = jnp.zeros((S, 128), F32)
@@ -357,7 +348,8 @@
             fars = [dot(t2[k % 2, k // 2], uq[128 * k : 128 * (k + 1), :]) for k in range(at, at + 8)]
             for k, far in zip(range(at, at + 8), fars):
                 for part in range(2):
-                    lanes = slice(256 * k + 128 * part, 256 * k + 128 * (part + 1))
+                    base = 512 * (k // 2) + 128 * (k % 2) + 256 * part
+                    lanes = slice(base, base + 128)
                     out = dst[:, lanes] + far[:, 128 * part : 128 * (part + 1)]
                     dst[:, lanes] = out
                     rd, bd, dd = rd + rv[:, lanes] * out, bd + bv[:, lanes] * out, dd + out * out
@@ -410,13 +402,13 @@
         expand_w(0, leaves // 16)
     mc_load.wait()
     with at("colA0"):
+        columns(0, home)
+    with at("mixA0"):
+        mix_columns(0, home)
+    with at("colB0"):
         columns(0, away)
-    with at("mixA0"):
+    with at("mixB0"):
         mix_columns(0, away)
-    with at("colB0"):
-        columns(0, home)
-    with at("mixB0"):
-        mix_columns(0, home)
     with at("expand_u"):
         u_load.wait()
         expand_u()
@@ -427,12 +419,13 @@
         spread_edges(0)
         near_edges(bv)
     with at("rowA0"):
+        rows(0, home)
+        mr_load.wait()
+        mix_rows_first(home)
+    with at("rowB0"):
         rows(0, away)
-    with at("rowB0"):
-        rows(0, home)
     with at("mixrow0"):
-        mr_load.wait()
-        mix_rows(0)
+        mix_rows(away)
     with at("expz0"):
         expand_and_compress(0, bv)
         send_edges(1, bv)
@@ -443,24 +436,25 @@
     with at("near1a"):
         near(dv, 8, 16)
     with at("colA1"):
+        columns(1, home)
+    with at("mixA1"):
+        mix_columns(1, home)
+    with at("colB1"):
         columns(1, away)
-    with at("mixA1"):
+    with at("mixB1"):
         mix_columns(1, away)
-    with at("colB1"):
-        columns(1, home)
-    with at("mixB1"):
-        mix_columns(1, home)
     with at("near1b"):
         near(dv, 24, inner - 16)
     with at("edges1"):
         spread_edges(1)
         near_edges(dv)
     with at("rowA1"):
+        rows(1, home)
+        mix_rows_first(home)
+    with at("rowB1"):
         rows(1, away)
-    with at("rowB1"):
-        rows(1, home)
     with at("mixrow1"):
-        mix_rows(1)
+        mix_rows(away)
     with at("expand1"):
         rd, bd, dd = last_expand(dv)
 
@@ -471,16 +465,17 @@
         for k in range(1, n_row):
             to = other_row(k)
             send(g1, h1.at[row], sent.at[3], h_sem.at[0], (to, col))
-        arrived(h1.at[pl.ds(0, n_row - 1)], h_sem.at[0])
+        with at("red1"):
+            arrived(h1.at[pl.ds(0, n_row - 1)], h_sem.at[0])
         packed = h1[0]
         for k in range(1, n_row):
             packed = packed + h1[k]
         g2[...] = packed
         h2[col] = packed
         for k in range(1, n_col):
-            to = other_col(k)
-            send(g2, h2.at[col], sent.at[4], h_sem.at[1], (row, to))
-        arrived(h2.at[pl.ds(0, n_col - 1)], h_sem.at[1])
+            send(g2, h2.at[col], sent.at[4], h_sem.at[1], (row, other_col(k)))
+        with at("red2"):
+            arrived(h2.at[pl.ds(0, n_col - 1)], h_sem.at[1])
         packed = h2[0]
         for k in range(1, n_col):
             packed = packed + h2[k]
@@ -518,19 +513,17 @@
 
 
 def finish(rv, bv, dv, coefs, sol_hbm, res_hbm, sol, res, sem):
-    sol_r, sol_b, res_r, res_b = (coefs[q] for q in range(4))
-    pieces = sem.shape[1]
-    width = rv.shape[1] // pieces
     copies = []
-    for piece in range(pieces):
-        for at in range(piece * width, (piece + 1) * width, 128):
+    for g in range(S // 8):
+        rows = slice(8 * g, 8 * (g + 1))
+        sol_r, sol_b, res_r, res_b = (coefs[q, rows] for q in range(4))
+        for at in range(0, rv.shape[1], 128):
             lanes = slice(at, at + 128)
-            r, b, d = rv[:, lanes], bv[:, lanes], dv[:, lanes]
-            sol[:, lanes] = sol_r * r + sol_b * b
-            res[:, lanes] = res_r * r - res_b * b - sol_b * d
-        lanes = pl.ds(piece * width, width)
+            r, b, d = rv[rows, lanes], bv[rows, lanes], dv[rows, lanes]
+            sol[rows, lanes] = sol_r * r + sol_b * b
+            res[rows, lanes] = res_r * r - res_b * b - sol_b * d
         for k, (src, dst) in enumerate(((sol, sol_hbm), (res, res_hbm))):
-            copies.append(pltpu.make_async_copy(src.at[:, lanes], dst.at[:, lanes], sem.at[k, piece]))
+            copies.append(pltpu.make_async_copy(src.at[rows], dst.at[rows], sem.at[k, g]))
             copies[-1].start()
     for copy in copies:
         copy.wait()
@@ -557,7 +550,7 @@
                 pltpu.VMEM((leaves * 128, 128), BF16),
                 pltpu.VMEM((leaves * 64, 256), BF16),
                 pltpu.VMEM((leaves * 16, 128), BF16),
-                pltpu.VMEM((leaves * 64, 128), BF16),
+                pltpu.VMEM((2, n_col, 256, 128), BF16),
                 pltpu.VMEM((leaves * 16, 128), BF16),
                 pltpu.VMEM((leaves * 32, 256), BF16),
                 pltpu.VMEM(mix_col.shape[1:], BF16),
@@ -572,8 +565,9 @@
                 pltpu.VMEM((2, n_row, 4, S, 128), BF16),
                 pltpu.VMEM((2, n_row, 4, S, 128), BF16),
                 pltpu.VMEM((n_col, 2, S, 128), BF16),
+                pltpu.VMEM((n_col, S, n_row * RANK), F32),
                 pltpu.VMEM((2, n_col, S, 128), BF16),
-                pltpu.VMEM((leaves * 16, 128), F32),
+                pltpu.VMEM((n_col, 128, 128), F32),
                 pltpu.VMEM((16, 128, 128), F32),
                 pltpu.VMEM((16, 128, 128), F32),
                 pltpu.VMEM((8, 128), F32),
@@ -602,7 +596,7 @@
             scratch_shapes=[
                 pltpu.VMEM((S, unknowns), F32),
                 pltpu.VMEM((S, unknowns), F32),
-                pltpu.SemaphoreType.DMA((2, 4)),
+                pltpu.SemaphoreType.DMA((2, S // 8)),
             ],
             compiler_params=pltpu.CompilerParams(vmem_limit_bytes=8 * 1024 * 1024),
         )(*(pltpu.with_memory_space_constraint(x, pltpu.VMEM) for x in parts))

time: 42.2 us -> 41.8 us (level)
    pallas_call x1, Pallas kernels: 40.1 us -> 39.6 us  [body(): pl.pallas_call(functools.partial(kernel, n_row, n_col), out_shape=[field,...]
where the time goes in v4:
time: 41.8 us; the launch traced here: 41.7 us
  Pallas kernels  41.1 us (98%)
  between operations  0.64 us (2%)
    pallas_call x1, Pallas kernels, body(): pl.pallas_call(functools.partial(kernel, n_row, n_col), out_shape=[field,...  39.6 us
    pallas_call x1, Pallas kernels, body(): pl.pallas_call(finish, out_shape=[jax.ShapeDtypeStruct((S, unknowns), F32...  1.42 us

profile of v4, /device:TPU:1, one launch (start us, length us, event | category | flops | bytes accessed | tf_op | source)
XLA Modules:
  0.0 41.7 jit_solution(13046840518947580895)
XLA Ops:
  0.6 39.6 %shard_map.86 = (f32[32,8192]{1,0:T(8,128)S(1)}, f32[32,8192]{1,0:T(8,128)S(1)}, f32[32,8192]{1,0:T(8,128)S(1)}, f32[4,32,128]{2,1,0:T(8,128)S(1)}) custom-call(f32[32,8192]{1,0:T(8,128)} %r_hbm.1, bf16[16384,128]{1,0:T(8,128)(2,1)} %bitcast.18, s32[4,128]{1,0:T(4,128)} %bitcast.23, bf16[2048,128]{1,0:T(8,128)(2,1)} %bitcast.21, ...), custom_call_target="tpu_custom_call" | custom-call | tf_op jit(solution)/shard_map/pallas_call | solution.py:543
  40.3 1.4 %shard_map.87 = (f32[32,8192]{1,0:T(8,128)}, f32[32,8192]{1,0:T(8,128)}) custom-call(f32[32,8192]{1,0:T(8,128)S(1)} %get-tuple-element.6.rv, f32[32,8192]{1,0:T(8,128)S(1)} %get-tuple-element.7.bv, f32[32,8192]{1,0:T(8,128)S(1)} %get-tuple-element.8.dv, f32[4,32,128]{2,1,0:T(8,128)S(1)} %get-tuple-element.9.coefs), custom_call_target="tpu_custom_call" | custom-call | tf_op jit(solution)/shard_map/pallas_call | solution.py:591

commit v5 on v4

--- a/solution.py
+++ b/solution.py
@@ -43,7 +43,7 @@
     r_hbm, w_hbm, off_hbm, v_hbm, mc_hbm, mr_hbm, u_hbm,
     rv, bv, dv, coefs,
     off, wraw, wp, vraw, vq, uraw, uq, mc, mr, xd, turn,
-    hs, hr, zs, zr, zt, ts, tr, tt, tp, t2, sv, sa, sb, g1, h1, g2, h2,
+    hs, hr, zs, zr, zt, ts, tr, tt, tp, t2, sv, sa, sb, g, h,
     load_sem, sent, hr_sem, zr_sem, tr_sem, h_sem,
 ):
     row = lax.axis_index("row")
@@ -303,19 +303,20 @@
 
     def mix_columns(app, half):
         to_rows = [2 * half + lax.rem(lax.rem(row, 2) + k, 2) + 4 * lax.rem(lax.div(row, 4) + m, 2) for m, k in ((1, 0), (1, 1), (0, 1), (0, 0))]
-        made = []
-        for j in to_rows:
-            z = jnp.concatenate([zt[j, c] for c in range(4)], axis=1)
-            made.append(dot(z, mc[j]).astype(BF16))
-        for at, (j, t) in enumerate(zip(to_rows, made)):
-            stays = half is home and at == 3
-            for p in range(4):
-                if stays:
-                    tr[app, row, p] = t[:, 128 * p : 128 * (p + 1)]
-                else:
-                    ts[app, j, p] = t[:, 128 * p : 128 * (p + 1)]
-            if not stays:
-                send(ts.at[app, j], tr.at[app, row], sent.at[2], tr_sem.at[app, at_half(half)], (j, col))
+        for first in (0, 2):
+            made = []
+            for j in to_rows[first : first + 2]:
+                z = jnp.concatenate([zt[j, c] for c in range(4)], axis=1)
+                made.append(dot(z, mc[j]).astype(BF16))
+            for at, j, t in zip((first, first + 1), to_rows[first:], made):
+                stays = half is home and at == 3
+                for p in range(4):
+                    if stays:
+                        tr[app, row, p] = t[:, 128 * p : 128 * (p + 1)]
+                    else:
+                        ts[app, j, p] = t[:, 128 * p : 128 * (p + 1)]
+                if not stays:
+                    send(ts.at[app, j], tr.at[app, row], sent.at[2], tr_sem.at[app, at_half(half)], (j, col))
 
     def rows(app, half):
         arrived(tr.at[app, pl.ds(0, 4 if half is away else 3)], tr_sem.at[app, at_half(half)])
@@ -460,25 +461,34 @@
 
     with at("reduce"):
         packed = placed(packed, (3, 4, 5), (rd, bd, dd))
-        g1[...] = packed
-        h1[row] = packed
-        for k in range(1, n_row):
-            to = other_row(k)
-            send(g1, h1.at[row], sent.at[3], h_sem.at[0], (to, col))
-        with at("red1"):
-            arrived(h1.at[pl.ds(0, n_row - 1)], h_sem.at[0])
-        packed = h1[0]
-        for k in range(1, n_row):
-            packed = packed + h1[k]
-        g2[...] = packed
-        h2[col] = packed
-        for k in range(1, n_col):
-            send(g2, h2.at[col], sent.at[4], h_sem.at[1], (row, other_col(k)))
-        with at("red2"):
-            arrived(h2.at[pl.ds(0, n_col - 1)], h_sem.at[1])
-        packed = h2[0]
-        for k in range(1, n_col):
-            packed = packed + h2[k]
+        line = lax.broadcasted_iota(jnp.int32, (8, 128), 0)
+
+        def by_line(shifts, x):
+            out = x
+            for k in range(1, 4):
+                out = jnp.where(lax.rem(line, 4) == k, pltpu.roll(x, shifts[k], 1), out)
+            return out
+
+        packed = by_line((0, 32, 64, 96), packed)
+        packed = packed + pltpu.roll(packed, 7, 0)
+        packed = packed + pltpu.roll(packed, 6, 0)
+        mine = jnp.concatenate([packed[0:1], packed[4:5]], axis=0)
+        g[...] = mine
+        h[flat] = mine
+        x_at = lax.div(row, 2)
+        far = lambda d: min(d, 4 - d)
+        ways = [(dx, dc, k) for dx in range(4) for dc in range(2) for k in range(n_col)]
+        ways.sort(key=lambda w: -far(w[0]) - far(steps[w[2]][0]) - far(steps[w[2]][1]) - 0.5 * w[1])
+        lines = {(dx, dc): 2 * lax.rem(x_at + dx, 4) + lax.rem(row + dc, 2) for dx in range(4) for dc in range(2)}
+        for dx, dc, k in ways[:-1]:
+            send(g, h.at[flat], sent.at[3], h_sem, (lines[dx, dc], order[k]))
+        with at("red"):
+            arrived(h.at[pl.ds(0, total - 1)], h_sem)
+        sums = [h[k] for k in range(4)]
+        for k in range(4, total):
+            sums[k % 4] = sums[k % 4] + h[k]
+        both = (sums[0] + sums[1]) + (sums[2] + sums[3])
+        packed = by_line((0, 96, 64, 32), jnp.where(line < 4, both[0:1], both[1:2]))
 
     with at("coefs"):
         rr, rb, bb, rd, bd, dd = (packed if q == 0 else pltpu.roll(packed, 128 - q, 1) for q in range(6))
@@ -508,8 +518,7 @@
         arrived(hs, sent.at[0])
         arrived(zs.at[:, :, pl.ds(0, n_col - 1)], sent.at[1])
         arrived(ts.at[:, pl.ds(0, n_row - 1)], sent.at[2])
-        arrived(h1.at[pl.ds(0, n_row - 1)], sent.at[3])
-        arrived(h2.at[pl.ds(0, n_col - 1)], sent.at[4])
+        arrived(h.at[pl.ds(0, total - 1)], sent.at[3])
 
 
 def finish(rv, bv, dv, coefs, sol_hbm, res_hbm, sol, res, sem):
@@ -570,16 +579,14 @@
                 pltpu.VMEM((n_col, 128, 128), F32),
                 pltpu.VMEM((16, 128, 128), F32),
                 pltpu.VMEM((16, 128, 128), F32),
-                pltpu.VMEM((8, 128), F32),
-                pltpu.VMEM((n_row, 8, 128), F32),
-                pltpu.VMEM((8, 128), F32),
-                pltpu.VMEM((n_col, 8, 128), F32),
+                pltpu.VMEM((2, 128), F32),
+                pltpu.VMEM((n_row * n_col, 2, 128), F32),
                 pltpu.SemaphoreType.DMA((5 + 2 * 4,)),
-                pltpu.SemaphoreType.DMA((5,)),
+                pltpu.SemaphoreType.DMA((4,)),
                 pltpu.SemaphoreType.DMA((2,)),
                 pltpu.SemaphoreType.DMA((2, 2)),
                 pltpu.SemaphoreType.DMA((2, 2)),
-                pltpu.SemaphoreType.DMA((2,)),
+                pltpu.SemaphoreType.DMA,
             ],
             compiler_params=pltpu.CompilerParams(
                 collective_id=0, has_side_effects=True, vmem_limit_bytes=54 * 1024 * 1024

time: 41.8 us -> 40.4 us (0.967)
  Pallas kernels: 41.1 us -> 39.7 us
    pallas_call x1, Pallas kernels: 39.6 us -> 38.2 us  [body(): pl.pallas_call(functools.partial(kernel, n_row, n_col), out_shape=[field,...]
where the time goes in v5:
time: 40.4 us; the launch traced here: 40.3 us
  Pallas kernels  39.7 us (98%)
  between operations  0.64 us (2%)
    pallas_call x1, Pallas kernels, body(): pl.pallas_call(functools.partial(kernel, n_row, n_col), out_shape=[field,...  38.2 us
    pallas_call x1, Pallas kernels, body(): pl.pallas_call(finish, out_shape=[jax.ShapeDtypeStruct((S, unknowns), F32...  1.42 us

profile of v5, /device:TPU:1, one launch (start us, length us, event | category | flops | bytes accessed | tf_op | source)
XLA Modules:
  0.0 40.3 jit_solution(379881777767002425)
XLA Ops:
  0.6 38.2 %shard_map.86 = (f32[32,8192]{1,0:T(8,128)S(1)}, f32[32,8192]{1,0:T(8,128)S(1)}, f32[32,8192]{1,0:T(8,128)S(1)}, f32[4,32,128]{2,1,0:T(8,128)S(1)}) custom-call(f32[32,8192]{1,0:T(8,128)} %r_hbm.1, bf16[16384,128]{1,0:T(8,128)(2,1)} %bitcast.18, s32[4,128]{1,0:T(4,128)} %bitcast.23, bf16[2048,128]{1,0:T(8,128)(2,1)} %bitcast.21, ...), custom_call_target="tpu_custom_call" | custom-call | tf_op jit(solution)/shard_map/pallas_call | solution.py:552
  38.9 1.4 %shard_map.87 = (f32[32,8192]{1,0:T(8,128)}, f32[32,8192]{1,0:T(8,128)}) custom-call(f32[32,8192]{1,0:T(8,128)S(1)} %get-tuple-element.6.rv, f32[32,8192]{1,0:T(8,128)S(1)} %get-tuple-element.7.bv, f32[32,8192]{1,0:T(8,128)S(1)} %get-tuple-element.8.dv, f32[4,32,128]{2,1,0:T(8,128)S(1)} %get-tuple-element.9.coefs), custom_call_target="tpu_custom_call" | custom-call | tf_op jit(solution)/shard_map/pallas_call | solution.py:598

commit v6 on v5

--- a/solution.py
+++ b/solution.py
@@ -59,6 +59,15 @@
         copy.start()
         return copy
 
+    for piece in range(4):
+        rows = pl.ds(piece * (leaves * 4), leaves * 4)
+        pltpu.make_async_copy(v_hbm.at[rows], vraw.at[rows], load_sem.at[5]).start()
+    for piece in range(4):
+        rows = pl.ds(piece * (S // 4), S // 4)
+        pltpu.make_async_copy(r_hbm.at[rows], rv.at[rows], load_sem.at[6]).start()
+    off_load = loads(0, off_hbm, off)
+    w_load = loads(1, w_hbm, wraw)
+
     col_slow, col_fast, row_fast = lax.div(col, 4), lax.rem(col, 4), lax.rem(row, 4)
     home = lax.rem(lax.div(row, 2), 2)
     away = 1 - home
@@ -74,21 +83,6 @@
 
     def at_half(half):
         return 0 if half is home else 1
-
-    for group in range(4):
-        for k in range(4 * group, 4 * (group + 1)):
-            to = order[k]
-            rows = pl.ds(pl.multiple_of(to * 128, 128), 128)
-            place = vraw.at[pl.ds(128 * k, 128)]
-            pltpu.make_async_copy(v_hbm.at[rows], place, load_sem.at[5 + 2 * group]).start()
-            lanes = pl.ds(pl.multiple_of(to * 512, 512), 512)
-            pltpu.make_async_copy(r_hbm.at[:, lanes], rv.at[:, lanes], load_sem.at[6 + 2 * group]).start()
-    off_load = loads(0, off_hbm, off)
-    w_load = loads(1, w_hbm, wraw)
-
-    def first_loads(group):
-        pltpu.make_async_copy(v_hbm.at[0:512], vraw.at[0:512], load_sem.at[5 + 2 * group]).wait()
-        pltpu.make_async_copy(r_hbm.at[:, 0:2048], rv.at[:, 0:2048], load_sem.at[6 + 2 * group]).wait()
 
     def other_col(k):
         return lax.rem(col + k, n_col)
@@ -214,10 +208,10 @@
         ks = list(range(n_col))
         for half in (home, away):
             if half is home:
-                for group in range(4):
-                    first_loads(group)
-                    for k in range(4 * group, 4 * group + 4):
-                        sv[k] = vraw[128 * k : 128 * (k + 1), :].astype(F32)
+                pltpu.make_async_copy(v_hbm, vraw, load_sem.at[5]).wait()
+                for k in ks:
+                    sv[k] = vraw[pl.ds(pl.multiple_of(order[k] * 128, 128), 128), :].astype(F32)
+                pltpu.make_async_copy(r_hbm, rv, load_sem.at[6]).wait()
             for k in ks:
                 expand_v(k, half)
             fields = turned_fields([field(rv, to, half) for to in order])
@@ -303,20 +297,19 @@
 
     def mix_columns(app, half):
         to_rows = [2 * half + lax.rem(lax.rem(row, 2) + k, 2) + 4 * lax.rem(lax.div(row, 4) + m, 2) for m, k in ((1, 0), (1, 1), (0, 1), (0, 0))]
-        for first in (0, 2):
-            made = []
-            for j in to_rows[first : first + 2]:
-                z = jnp.concatenate([zt[j, c] for c in range(4)], axis=1)
-                made.append(dot(z, mc[j]).astype(BF16))
-            for at, j, t in zip((first, first + 1), to_rows[first:], made):
-                stays = half is home and at == 3
-                for p in range(4):
-                    if stays:
-                        tr[app, row, p] = t[:, 128 * p : 128 * (p + 1)]
-                    else:
-                        ts[app, j, p] = t[:, 128 * p : 128 * (p + 1)]
-                if not stays:
-                    send(ts.at[app, j], tr.at[app, row], sent.at[2], tr_sem.at[app, at_half(half)], (j, col))
+        made = []
+        for j in to_rows:
+            z = jnp.concatenate([zt[j, c] for c in range(4)], axis=1)
+            made.append(dot(z, mc[j]).astype(BF16))
+        for at, (j, t) in enumerate(zip(to_rows, made)):
+            stays = half is home and at == 3
+            for p in range(4):
+                if stays:
+                    tr[app, row, p] = t[:, 128 * p : 128 * (p + 1)]
+                else:
+                    ts[app, j, p] = t[:, 128 * p : 128 * (p + 1)]
+            if not stays:
+                send(ts.at[app, j], tr.at[app, row], sent.at[2], tr_sem.at[app, at_half(half)], (j, col))
 
     def rows(app, half):
         arrived(tr.at[app, pl.ds(0, 4 if half is away else 3)], tr_sem.at[app, at_half(half)])
@@ -522,20 +515,21 @@
 
 
 def finish(rv, bv, dv, coefs, sol_hbm, res_hbm, sol, res, sem):
-    copies = []
+    width = rv.shape[1] // 2
     for g in range(S // 8):
         rows = slice(8 * g, 8 * (g + 1))
         sol_r, sol_b, res_r, res_b = (coefs[q, rows] for q in range(4))
-        for at in range(0, rv.shape[1], 128):
-            lanes = slice(at, at + 128)
-            r, b, d = rv[rows, lanes], bv[rows, lanes], dv[rows, lanes]
-            sol[rows, lanes] = sol_r * r + sol_b * b
-            res[rows, lanes] = res_r * r - res_b * b - sol_b * d
-        for k, (src, dst) in enumerate(((sol, sol_hbm), (res, res_hbm))):
-            copies.append(pltpu.make_async_copy(src.at[rows], dst.at[rows], sem.at[k, g]))
-            copies[-1].start()
-    for copy in copies:
-        copy.wait()
+        for part in range(2):
+            for at in range(part * width, (part + 1) * width, 128):
+                lanes = slice(at, at + 128)
+                r, b, d = rv[rows, lanes], bv[rows, lanes], dv[rows, lanes]
+                sol[rows, lanes] = sol_r * r + sol_b * b
+                res[rows, lanes] = res_r * r - res_b * b - sol_b * d
+            lanes = pl.ds(part * width, width)
+            for k, (src, dst) in enumerate(((sol, sol_hbm), (res, res_hbm))):
+                pltpu.make_async_copy(src.at[rows, lanes], dst.at[rows, lanes], sem.at[k]).start()
+    for k, (src, dst) in enumerate(((sol, sol_hbm), (res, res_hbm))):
+        pltpu.make_async_copy(src, dst, sem.at[k]).wait()
 
 
 def solution(mesh):
@@ -581,7 +575,7 @@
                 pltpu.VMEM((16, 128, 128), F32),
                 pltpu.VMEM((2, 128), F32),
                 pltpu.VMEM((n_row * n_col, 2, 128), F32),
-                pltpu.SemaphoreType.DMA((5 + 2 * 4,)),
+                pltpu.SemaphoreType.DMA((7,)),
                 pltpu.SemaphoreType.DMA((4,)),
                 pltpu.SemaphoreType.DMA((2,)),
                 pltpu.SemaphoreType.DMA((2, 2)),
@@ -603,7 +597,7 @@
             scratch_shapes=[
                 pltpu.VMEM((S, unknowns), F32),
                 pltpu.VMEM((S, unknowns), F32),
-                pltpu.SemaphoreType.DMA((2, S // 8)),
+                pltpu.SemaphoreType.DMA((2,)),
             ],
             compiler_params=pltpu.CompilerParams(vmem_limit_bytes=8 * 1024 * 1024),
         )(*(pltpu.with_memory_space_constraint(x, pltpu.VMEM) for x in parts))

time: 40.4 us -> 40.4 us (level)
  no operation moved by 1% of the time
where the time goes in v6:
time: 40.4 us; the launch traced here: 40.3 us
  Pallas kernels  39.7 us (98%)
  between operations  0.64 us (2%)
    pallas_call x1, Pallas kernels, body(): pl.pallas_call(functools.partial(kernel, n_row, n_col), out_shape=[field,...  38.4 us
    pallas_call x1, Pallas kernels, body(): pl.pallas_call(finish, out_shape=[jax.ShapeDtypeStruct((S, unknowns), F32...  1.33 us

profile of v6, /device:TPU:1, one launch (start us, length us, event | category | flops | bytes accessed | tf_op | source)
XLA Modules:
  0.0 40.3 jit_solution(53644673288704838)
XLA Ops:
  0.6 38.4 %shard_map.86 = (f32[32,8192]{1,0:T(8,128)S(1)}, f32[32,8192]{1,0:T(8,128)S(1)}, f32[32,8192]{1,0:T(8,128)S(1)}, f32[4,32,128]{2,1,0:T(8,128)S(1)}) custom-call(f32[32,8192]{1,0:T(8,128)} %r_hbm.1, bf16[16384,128]{1,0:T(8,128)(2,1)} %bitcast.18, s32[4,128]{1,0:T(4,128)} %bitcast.23, bf16[2048,128]{1,0:T(8,128)(2,1)} %bitcast.21, ...), custom_call_target="tpu_custom_call" | custom-call | tf_op jit(solution)/shard_map/pallas_call | solution.py:546
  39.0 1.3 %shard_map.87 = (f32[32,8192]{1,0:T(8,128)}, f32[32,8192]{1,0:T(8,128)}) custom-call(f32[32,8192]{1,0:T(8,128)S(1)} %get-tuple-element.6.rv, f32[32,8192]{1,0:T(8,128)S(1)} %get-tuple-element.7.bv, f32[32,8192]{1,0:T(8,128)S(1)} %get-tuple-element.8.dv, f32[4,32,128]{2,1,0:T(8,128)S(1)} %get-tuple-element.9.coefs), custom_call_target="tpu_custom_call" | custom-call | tf_op jit(solution)/shard_map/pallas_call | solution.py:592

commit v7 on v6

--- a/solution.py
+++ b/solution.py
@@ -178,8 +178,8 @@
     def send_edges(app, src):
         hs[app, 0] = src[:, 0 : HALO * LEAF].astype(BF16)
         hs[app, 1] = src[:, (leaves - HALO) * LEAF : leaves * LEAF].astype(BF16)
-        send(hs.at[app, 0], hr.at[app, 1], sent.at[0], hr_sem.at[app], down)
-        send(hs.at[app, 1], hr.at[app, 0], sent.at[0], hr_sem.at[app], up)
+        send(hs.at[app, 0], hr.at[app, 1], sent, hr_sem.at[app], down)
+        send(hs.at[app, 1], hr.at[app, 0], sent, hr_sem.at[app], up)
 
     def field(src, to, half):
         return jnp.concatenate([src[:, lanes] for lanes in tiles_of(to, half)], axis=1)
@@ -199,7 +199,7 @@
                 zs[app, h, k] = z
         for k in ks:
             if k < n_col - 1:
-                send(zs.at[app, h, k], zr.at[app, half, col], sent.at[1], zr_sem.at[app, h], (row, order[k]))
+                send(zs.at[app, h, k], zr.at[app, half, col], sent, zr_sem.at[app, h], (row, order[k]))
 
     def tiles_of(to, half):
         return [pl.ds(pl.multiple_of(to * 512 + half * 128 + part * 256, 128), 128) for part in range(2)]
@@ -309,7 +309,7 @@
                 else:
                     ts[app, j, p] = t[:, 128 * p : 128 * (p + 1)]
             if not stays:
-                send(ts.at[app, j], tr.at[app, row], sent.at[2], tr_sem.at[app, at_half(half)], (j, col))
+                send(ts.at[app, j], tr.at[app, row], sent, tr_sem.at[app, at_half(half)], (j, col))
 
     def rows(app, half):
         arrived(tr.at[app, pl.ds(0, 4 if half is away else 3)], tr_sem.at[app, at_half(half)])
@@ -474,7 +474,7 @@
         ways.sort(key=lambda w: -far(w[0]) - far(steps[w[2]][0]) - far(steps[w[2]][1]) - 0.5 * w[1])
         lines = {(dx, dc): 2 * lax.rem(x_at + dx, 4) + lax.rem(row + dc, 2) for dx in range(4) for dc in range(2)}
         for dx, dc, k in ways[:-1]:
-            send(g, h.at[flat], sent.at[3], h_sem, (lines[dx, dc], order[k]))
+            send(g, h.at[flat], sent, h_sem, (lines[dx, dc], order[k]))
         with at("red"):
             arrived(h.at[pl.ds(0, total - 1)], h_sem)
         sums = [h[k] for k in range(4)]
@@ -508,10 +508,8 @@
                 coefs[q, 8 * g : 8 * (g + 1)] = jnp.broadcast_to(x[:, 8 * g : 8 * g + 1], (8, 128))
 
     with at("drain"):
-        arrived(hs, sent.at[0])
-        arrived(zs.at[:, :, pl.ds(0, n_col - 1)], sent.at[1])
-        arrived(ts.at[:, pl.ds(0, n_row - 1)], sent.at[2])
-        arrived(h.at[pl.ds(0, total - 1)], sent.at[3])
+        edges, zs_, ts_, gs = 4 * S * HALO * LEAF, 4 * (n_col - 1) * S * 128, 2 * (n_row - 1) * S * n_col * RANK, (total - 1) * 512
+        arrived(wraw.at[pl.ds(0, (edges + zs_ + ts_ + gs) // 128)], sent)
 
 
 def finish(rv, bv, dv, coefs, sol_hbm, res_hbm, sol, res, sem):
@@ -576,7 +574,7 @@
                 pltpu.VMEM((2, 128), F32),
                 pltpu.VMEM((n_row * n_col, 2, 128), F32),
                 pltpu.SemaphoreType.DMA((7,)),
-                pltpu.SemaphoreType.DMA((4,)),
+                pltpu.SemaphoreType.DMA,
                 pltpu.SemaphoreType.DMA((2,)),
                 pltpu.SemaphoreType.DMA((2, 2)),
                 pltpu.SemaphoreType.DMA((2, 2)),

time: 40.4 us -> 40.4 us (level)
  no operation moved by 1% of the time
where the time goes in v7:
time: 40.4 us; the launch traced here: 40.3 us
  Pallas kernels  39.7 us (98%)
  between operations  0.64 us (2%)
    pallas_call x1, Pallas kernels, body(): pl.pallas_call(functools.partial(kernel, n_row, n_col), out_shape=[field,...  38.3 us
    pallas_call x1, Pallas kernels, body(): pl.pallas_call(finish, out_shape=[jax.ShapeDtypeStruct((S, unknowns), F32...  1.33 us

profile of v7, /device:TPU:1, one launch (start us, length us, event | category | flops | bytes accessed | tf_op | source)
XLA Modules:
  0.0 40.3 jit_solution(14860625777514646577)
XLA Ops:
  0.6 38.3 %shard_map.86 = (f32[32,8192]{1,0:T(8,128)S(1)}, f32[32,8192]{1,0:T(8,128)S(1)}, f32[32,8192]{1,0:T(8,128)S(1)}, f32[4,32,128]{2,1,0:T(8,128)S(1)}) custom-call(f32[32,8192]{1,0:T(8,128)} %r_hbm.1, bf16[16384,128]{1,0:T(8,128)(2,1)} %bitcast.18, s32[4,128]{1,0:T(4,128)} %bitcast.23, bf16[2048,128]{1,0:T(8,128)(2,1)} %bitcast.21, ...), custom_call_target="tpu_custom_call" | custom-call | tf_op jit(solution)/shard_map/pallas_call | solution.py:544
  39.0 1.3 %shard_map.87 = (f32[32,8192]{1,0:T(8,128)}, f32[32,8192]{1,0:T(8,128)}) custom-call(f32[32,8192]{1,0:T(8,128)S(1)} %get-tuple-element.6.rv, f32[32,8192]{1,0:T(8,128)S(1)} %get-tuple-element.7.bv, f32[32,8192]{1,0:T(8,128)S(1)} %get-tuple-element.8.dv, f32[4,32,128]{2,1,0:T(8,128)S(1)} %get-tuple-element.9.coefs), custom_call_target="tpu_custom_call" | custom-call | tf_op jit(solution)/shard_map/pallas_call | solution.py:590
